TPU v7x, 32 devices: a whole 2x2x4 slice. The times are simulated.
32 devices in a mesh: wide: 4 (over y, x), narrow: 8 (over z, core).
Axes of the slice: x: 2, y: 2, z: 4, core: 2. Of those that a mesh axis runs over, the one named last changes fastest.
Arguments:
- right_side: float32 [64, 32768], P(None, ('wide', 'narrow'))
- leaf_blocks: float32 [32768, 1024], P(('wide', 'narrow')), as said below
- factors: float32 [5, 64, 32768], P(None, None, ('wide', 'narrow'))
- leaf_order: int32 [32768], P(('wide', 'narrow')), may hold values from 0 to 32767, as said below
Outputs:
- solution: float32 [64, 32768], P(None, ('wide', 'narrow'))
- residual: float32 [64, 32768], P(None, ('wide', 'narrow'))
Inputs may be any that keep to these rules, and one draw needn't show every extreme that they name: `leaf_order`: each aligned block of 1024 entries is a permutation of the indices of that same block. `leaf_blocks`: each leaf block is symmetric.
All inputs are finite; a program needn't handle non-finite values.
Results may differ from a plain program's by a relative error of at most 0.0003.
Values sent between devices are 32-bit elements; how exact they have to be, the bound alone decides.
No kernel may reach another device: no remote copies, remote signals or barrier semaphores. Data moves between devices by JAX's collectives and lax.ppermute only.
A program may use at most 64 MiB of HBM per device.

v0:
```python
import jax
import jax.numpy as jnp
from jax import lax
from jax.sharding import PartitionSpec as P

ITERS = 2


HIGH = lax.Precision.HIGHEST


def swapped(value, axis, stride):
    mask = 2**stride
    pairs = [(source, source ^ mask) for source in range(lax.axis_size(axis))]
    return lax.ppermute(value, axis, pairs)


def butterfly_sums(projected, partial_value):
    low_levels = lax.axis_size("narrow").bit_length() - 1
    levels = projected.shape[0]
    running = projected
    totals = partial_value
    found = []
    for level in range(levels):
        if level < low_levels:
            partner, other = swapped((running, totals), "narrow", level)
        else:
            partner, other = swapped((running, totals), "wide", level - low_levels)
        cross = 2.0 * jnp.sum(running[0] * partner[0], axis=1)
        totals = totals + other + jnp.stack([jnp.zeros_like(cross), cross])
        found.append(partner[0])
        running = (running + partner)[1:]
    return (jnp.stack(found), totals)


def kernel_with_sums(vector, leaf_blocks, factors):
    near = jnp.dot(vector, leaf_blocks, precision=HIGH, preferred_element_type=jnp.float32)
    projected = jnp.einsum("rl,kql->krq", vector, factors, precision=HIGH)
    partial_value = jnp.stack([jnp.sum(vector * vector, axis=1), jnp.sum(vector * near, axis=1)])
    sibling, totals = butterfly_sums(projected, partial_value)
    far = jnp.einsum("krq,kql->rl", sibling, factors, precision=HIGH)
    return (near + far, totals[0], totals[1])


def local(right_side, leaf_blocks, factors, leaf_order):
    leaf_width = leaf_blocks.shape[1]
    leaf_index = lax.axis_index("wide") * lax.axis_size("narrow") + lax.axis_index("narrow")
    local_order = leaf_order - leaf_index * leaf_width
    rhs_leaf = jnp.take(right_side, local_order, axis=1)
    solution = jnp.zeros_like(rhs_leaf)
    residual = rhs_leaf
    image, norm_now, product = kernel_with_sums(residual, leaf_blocks, factors)
    alpha = norm_now / product
    direction = residual
    along = image
    for step in range(ITERS):
        solution = solution + alpha[:, None] * direction
        residual = residual - alpha[:, None] * along
        if step + 1 < ITERS:
            image, norm_next, product = kernel_with_sums(residual, leaf_blocks, factors)
            ratio = norm_next / norm_now
            alpha = norm_next / (product - ratio * norm_next / alpha)
            direction = residual + ratio[:, None] * direction
            along = image + ratio[:, None] * along
            norm_now = norm_next
    placed_sol = jnp.zeros_like(right_side).at[:, local_order].set(solution)
    placed_res = jnp.zeros_like(right_side).at[:, local_order].set(residual)
    return (placed_sol, placed_res)


def solution(mesh):
    placed = (
        P(None, ("wide", "narrow")),
        P(("wide", "narrow"), None),
        P(None, None, ("wide", "narrow")),
        P(("wide", "narrow")),
    )
    return jax.shard_map(
        local,
        mesh=mesh,
        in_specs=placed,
        out_specs=(P(None, ("wide", "narrow")), P(None, ("wide", "narrow"))),
        check_vma=False,
    )
```

profile of v0, /device:TPU:0, one launch (start us, length us, event | category | flops | bytes accessed | tf_op | source)
XLA Modules:
  0.0 75.4 jit_solution(9419735601759971093)
XLA Ops:
  0.7 0.8 %compare_and_fusion = (pred[1024]{0:T(1024)(128)(4,1)S(1)}, s32[1024]{0:T(1024)S(1)}) fusion(s32[1024]{0:T(1024)} %param.7, s32[]{:T(128)S(6)} %mul.238), kind=kLoop, calls=%fused_computation.70 | loop fusion | flops 7168 | bytes 9220 | tf_op jit(solution)/shard_map/jit(_take)/and | solution.py:49
  1.5 1.1 %copy.6 = f32[64,1024]{0,1:T(8,128)S(1)} copy(f32[64,1024]{1,0:T(8,128)} %param.4) | data formatting | bytes 524288 | tf_op args[0]
  2.6 2.8 %gather_fusion = f32[1024,64]{1,0:T(8,128)S(1)} fusion(f32[64,1024]{0,1:T(8,128)S(1)} %copy.6, s32[1024]{0:T(1024)S(1)} %broadcast_clamp_fusion), kind=kCustom, calls=%fused_computation | custom fusion | bytes 528384 | tf_op jit(solution)/shard_map/jit(_take)/gather | solution.py:49
  5.4 0.2 copy.7
  5.6 1.2 %convolution_bitcast_fusion.3 = f32[5,64,64]{1,2,0:T(8,128)S(1)} fusion(f32[5,64,1024]{2,1,0:T(8,128)S(1)} %copy-done, f32[1024,64]{0,1:T(8,128)S(1)} %copy.7, pred[1024]{0:T(1024)(128)(4,1)S(1)} %get-tuple-element.10), kind=kOutput, calls=%fused_computation.12 | convolution fusion | flops 251723776 | bytes 1655808 | tf_op jit(solution)/shard_map/rl,kql->krq/dot_general | solution.py:38
  6.8 0.6 collective-permute-start.1
  7.4 4.9 %fusion.8 = (f32[64]{0:T(128)S(1)}, f32[64]{0:T(128)S(1)}, f32[64,1024]{1,0:T(8,128)S(1)}) fusion(f32[1024,64]{0,1:T(8,128)S(1)} %copy.7, pred[1024]{0:T(1024)(128)(4,1)S(1)} %get-tuple-element.10, f32[1024,1024]{1,0:T(8,128)} %param.5), kind=kOutput, calls=%fused_computation.20 | convolution fusion | flops 805699456 | bytes 4720128 | tf_op jit(solution)/shard_map/dot_general | solution.py:37
  12.3 0.1 collective-permute-start
  12.5 3.1 %collective-permute-start.3 = (f32[4,64,64]{1,2,0:T(8,128)S(1)}, f32[4,64,64]{1,2,0:T(8,128)S(1)}, u32[]{:S(2)}, u32[]{:S(2)}) collective-permute-start(f32[4,64,64]{1,2,0:T(8,128)S(1)} %slice.131), channel_id=1, source_target_pairs={{0,2},{1,3},{2,0},{3,1},{4,6},{5,7},{6,4},{7,5},{8,10},{9,11},{10,... | collective-permute-start | bytes 196616 | tf_op jit(solution)/shard_map/ppermute | solution.py:15
  15.6 0.7 collective-permute-start.2
  16.4 2.9 %collective-permute-done.3 = f32[4,64,64]{1,2,0:T(8,128)S(1)} collective-permute-done((f32[4,64,64]{1,2,0:T(8,128)S(1)}, f32[4,64,64]{1,2,0:T(8,128)S(1)}, u32[]{:S(2)}, u32[]{:S(2)}) %collective-permute-start.3) | collective-permute-done | bytes 65568 | tf_op jit(solution)/shard_map/ppermute | solution.py:15
  19.4 2.8 %collective-permute-start.5 = (f32[3,64,64]{1,2,0:T(8,128)S(1)}, f32[3,64,64]{1,2,0:T(8,128)S(1)}, u32[]{:S(2)}, u32[]{:S(2)}) collective-permute-start(f32[3,64,64]{1,2,0:T(8,128)S(1)} %slice.134), channel_id=1, source_target_pairs={{0,4},{1,5},{2,6},{3,7},{4,0},{5,1},{6,2},{7,3},{8,12},{9,13},{10,... | collective-permute-start | bytes 147464 | tf_op jit(solution)/shard_map/ppermute | solution.py:15
  22.2 0.2 collective-permute-start.4
  22.4 4.2 %collective-permute-done.5 = f32[3,64,64]{1,2,0:T(8,128)S(1)} collective-permute-done((f32[3,64,64]{1,2,0:T(8,128)S(1)}, f32[3,64,64]{1,2,0:T(8,128)S(1)}, u32[]{:S(2)}, u32[]{:S(2)}) %collective-permute-start.5) | collective-permute-done | bytes 49184 | tf_op jit(solution)/shard_map/ppermute | solution.py:15
  26.7 1.4 %collective-permute-start.7 = (f32[2,64,64]{1,2,0:T(8,128)S(1)}, f32[2,64,64]{1,2,0:T(8,128)S(1)}, u32[]{:S(2)}, u32[]{:S(2)}) collective-permute-start(f32[2,64,64]{1,2,0:T(8,128)S(1)} %slice.137), channel_id=1, source_target_pairs={{0,8},{8,0},{16,24},{24,16},{1,9},{9,1},{17,25},{25,17},{2,10},{10... | collective-permute-start | bytes 98312 | tf_op jit(solution)/shard_map/ppermute | solution.py:15
  28.1 0.7 collective-permute-start.6
  28.8 2.2 %collective-permute-done.7 = f32[2,64,64]{1,2,0:T(8,128)S(1)} collective-permute-done((f32[2,64,64]{1,2,0:T(8,128)S(1)}, f32[2,64,64]{1,2,0:T(8,128)S(1)}, u32[]{:S(2)}, u32[]{:S(2)}) %collective-permute-start.7) | collective-permute-done | bytes 32800 | tf_op jit(solution)/shard_map/ppermute | solution.py:15
  31.0 1.5 %collective-permute-start.9 = (f32[1,64,64]{1,2,0:T(8,128)S(1)}, f32[1,64,64]{1,2,0:T(8,128)S(1)}, u32[]{:S(2)}, u32[]{:S(2)}) collective-permute-start(f32[1,64,64]{1,2,0:T(8,128)S(1)} %get-tuple-element.29), channel_id=1, source_target_pairs={{0,16},{8,24},{16,0},{24,8},{1,17},{9,25},{17,1},{25,9},{2,18},{10... | collective-permute-start | bytes 49160 | tf_op jit(solution)/shard_map/ppermute | solution.py:15
  32.5 0.8 %collective-permute-start.8 = (f32[2,64]{1,0:T(2,128)S(1)}, f32[2,64]{1,0:T(2,128)S(1)}, u32[]{:S(2)}, u32[]{:S(2)}) collective-permute-start(f32[2,64]{1,0:T(2,128)S(1)} %pad_add_fusion.6), channel_id=1, source_target_pairs={{0,16},{8,24},{16,0},{24,8},{1,17},{9,25},{17,1},{25,9},{2,18},{10... | collective-permute-start | bytes 1544 | tf_op jit(solution)/shard_map/ppermute | solution.py:15
  33.3 1.7 %collective-permute-done.9 = f32[1,64,64]{1,2,0:T(8,128)S(1)} collective-permute-done((f32[1,64,64]{1,2,0:T(8,128)S(1)}, f32[1,64,64]{1,2,0:T(8,128)S(1)}, u32[]{:S(2)}, u32[]{:S(2)}) %collective-permute-start.9) | collective-permute-done | bytes 16416 | tf_op jit(solution)/shard_map/ppermute | solution.py:15
  35.0 1.1 %collective-permute-done.8 = f32[2,64]{1,0:T(2,128)S(1)} collective-permute-done((f32[2,64]{1,0:T(2,128)S(1)}, f32[2,64]{1,0:T(2,128)S(1)}, u32[]{:S(2)}, u32[]{:S(2)}) %collective-permute-start.8) | collective-permute-done | bytes 544 | tf_op jit(solution)/shard_map/ppermute | solution.py:15
  36.2 1.0 %bitcast_subtract_fusion = (f32[64,1024]{1,0:T(8,128)S(1)}, f32[64,1024]{1,0:T(8,128)S(1)}) fusion(f32[1024,64]{0,1:T(8,128)S(1)} %copy.7, f32[64]{0:T(128)S(1)} %bitcast_divide_fusion.1, pred[1024]{0:T(1024)(128)(4,1)S(1)} %get-tuple-element.10, f32[64,1024]{1,0:T(8,128)S(1)} %get-tuple-element.34, f32[5,64,64]{1,2,0:T(8,128)S(1)} %get-tuple-element.33, ...), kind=kOutput, calls=%fused_computation.16 | convolution fusion | flops 251920384 | bytes 2442496 | tf_op jit(solution)/shard_map/krq,kql->rl/dot_general | solution.py:41
  37.2 1.2 %convolution_bitcast_fusion.2 = f32[5,64,64]{1,2,0:T(8,128)S(1)} fusion(f32[5,64,1024]{2,1,0:T(8,128)S(1)} %copy-done, f32[64,1024]{1,0:T(8,128)S(1)} %get-tuple-element.35), kind=kOutput, calls=%fused_computation.11 | convolution fusion | flops 251658240 | bytes 1654784 | tf_op jit(solution)/shard_map/rl,kql->krq/dot_general | solution.py:38
  38.4 2.8 %multiply_reduce_fusion.1 = (f32[64]{0:T(128)S(1)}, f32[64]{0:T(128)S(1)}, f32[64,1024]{1,0:T(8,128)S(1)}) fusion(f32[64,1024]{1,0:T(8,128)S(1)} %get-tuple-element.35, f32[1024,1024]{1,0:T(8,128)S(1)} %copy-done.1), kind=kOutput, calls=%fused_computation.27 | convolution fusion | flops 805568384 | bytes 4719104 | tf_op jit(solution)/shard_map/dot_general | solution.py:37
  41.2 0.5 collective-permute-start.10
  41.7 0.9 %collective-permute-done.11 = f32[5,64,64]{1,2,0:T(8,128)S(1)} collective-permute-done((f32[5,64,64]{1,2,0:T(8,128)S(1)}, f32[5,64,64]{1,2,0:T(8,128)S(1)}, u32[]{:S(2)}, u32[]{:S(2)}) %collective-permute-start.11) | collective-permute-done | bytes 81952 | tf_op jit(solution)/shard_map/ppermute | solution.py:15
  42.7 0.7 collective-permute-start.13
  43.4 1.4 %collective-permute-start.12 = (f32[2,64]{1,0:T(2,128)S(1)}, f32[2,64]{1,0:T(2,128)S(1)}, u32[]{:S(2)}, u32[]{:S(2)}) collective-permute-start(f32[2,64]{1,0:T(2,128)S(1)} %pad_add_fusion.4), channel_id=1, source_target_pairs={{0,2},{1,3},{2,0},{3,1},{4,6},{5,7},{6,4},{7,5},{8,10},{9,11},{10,... | collective-permute-start | bytes 1544 | tf_op jit(solution)/shard_map/ppermute | solution.py:15
  44.9 3.4 %collective-permute-done.13 = f32[4,64,64]{1,2,0:T(8,128)S(1)} collective-permute-done((f32[4,64,64]{1,2,0:T(8,128)S(1)}, f32[4,64,64]{1,2,0:T(8,128)S(1)}, u32[]{:S(2)}, u32[]{:S(2)}) %collective-permute-start.13) | collective-permute-done | bytes 65568 | tf_op jit(solution)/shard_map/ppermute | solution.py:15
  48.4 2.4 %collective-permute-start.15 = (f32[3,64,64]{1,2,0:T(8,128)S(1)}, f32[3,64,64]{1,2,0:T(8,128)S(1)}, u32[]{:S(2)}, u32[]{:S(2)}) collective-permute-start(f32[3,64,64]{1,2,0:T(8,128)S(1)} %slice.147), channel_id=1, source_target_pairs={{0,4},{1,5},{2,6},{3,7},{4,0},{5,1},{6,2},{7,3},{8,12},{9,13},{10,... | collective-permute-start | bytes 147464 | tf_op jit(solution)/shard_map/ppermute | solution.py:15
  50.8 0.7 collective-permute-start.14
  51.5 4.0 %collective-permute-done.15 = f32[3,64,64]{1,2,0:T(8,128)S(1)} collective-permute-done((f32[3,64,64]{1,2,0:T(8,128)S(1)}, f32[3,64,64]{1,2,0:T(8,128)S(1)}, u32[]{:S(2)}, u32[]{:S(2)}) %collective-permute-start.15) | collective-permute-done | bytes 49184 | tf_op jit(solution)/shard_map/ppermute | solution.py:15
  55.5 1.6 %collective-permute-start.17 = (f32[2,64,64]{1,2,0:T(8,128)S(1)}, f32[2,64,64]{1,2,0:T(8,128)S(1)}, u32[]{:S(2)}, u32[]{:S(2)}) collective-permute-start(f32[2,64,64]{1,2,0:T(8,128)S(1)} %slice.150), channel_id=1, source_target_pairs={{0,8},{8,0},{16,24},{24,16},{1,9},{9,1},{17,25},{25,17},{2,10},{10... | collective-permute-start | bytes 98312 | tf_op jit(solution)/shard_map/ppermute | solution.py:15
  57.1 0.6 collective-permute-start.16
  57.7 2.2 %collective-permute-done.17 = f32[2,64,64]{1,2,0:T(8,128)S(1)} collective-permute-done((f32[2,64,64]{1,2,0:T(8,128)S(1)}, f32[2,64,64]{1,2,0:T(8,128)S(1)}, u32[]{:S(2)}, u32[]{:S(2)}) %collective-permute-start.17) | collective-permute-done | bytes 32800 | tf_op jit(solution)/shard_map/ppermute | solution.py:15
  59.9 0.8 %collective-permute-start.19 = (f32[1,64,64]{1,2,0:T(8,128)S(1)}, f32[1,64,64]{1,2,0:T(8,128)S(1)}, u32[]{:S(2)}, u32[]{:S(2)}) collective-permute-start(f32[1,64,64]{1,2,0:T(8,128)S(1)} %get-tuple-element.25), channel_id=1, source_target_pairs={{0,16},{8,24},{16,0},{24,8},{1,17},{9,25},{17,1},{25,9},{2,18},{10... | collective-permute-start | bytes 49160 | tf_op jit(solution)/shard_map/ppermute | solution.py:15
  60.7 1.3 %collective-permute-start.18 = (f32[2,64]{1,0:T(2,128)S(1)}, f32[2,64]{1,0:T(2,128)S(1)}, u32[]{:S(2)}, u32[]{:S(2)}) collective-permute-start(f32[2,64]{1,0:T(2,128)S(1)} %pad_add_fusion.1), channel_id=1, source_target_pairs={{0,16},{8,24},{16,0},{24,8},{1,17},{9,25},{17,1},{25,9},{2,18},{10... | collective-permute-start | bytes 1544 | tf_op jit(solution)/shard_map/ppermute | solution.py:15
  62.0 1.8 %collective-permute-done.19 = f32[1,64,64]{1,2,0:T(8,128)S(1)} collective-permute-done((f32[1,64,64]{1,2,0:T(8,128)S(1)}, f32[1,64,64]{1,2,0:T(8,128)S(1)}, u32[]{:S(2)}, u32[]{:S(2)}) %collective-permute-start.19) | collective-permute-done | bytes 16416 | tf_op jit(solution)/shard_map/ppermute | solution.py:15
  63.9 0.5 collective-permute-done.18
  64.4 0.2 copy-done.2
  64.5 0.1 fusion.12
  64.7 0.2 copy.9
  64.9 3.4 %scatter_custom_fusion = f32[64,1024]{0,1:T(8,128)S(1)} fusion(s32[1024]{0:T(1024)S(1)} %get-tuple-element.11, f32[1024,64]{1,0:T(8,128)S(1)} %copy.9, f32[]{:T(128)} %constant.9.clone.1), kind=kCustom, calls=%fused_computation.30 | custom fusion | bytes 262148 | tf_op jit(solution)/shard_map/scatter | solution.py:66
  68.3 0.9 %copy.12 = f32[64,1024]{1,0:T(8,128)} copy(f32[64,1024]{0,1:T(8,128)S(1)} %scatter_custom_fusion) | data formatting | bytes 524288
  69.2 1.9 %fusion.4 = f32[1024,64]{0,1:T(8,128)S(1)} fusion(f32[64,1024]{1,0:T(8,128)S(1)} %get-tuple-element.35, f32[64,1024]{1,0:T(8,128)S(1)} %get-tuple-element.37, f32[5,64,64]{1,2,0:T(8,128)} %copy-done.2, f32[5,64,1024]{2,1,0:T(8,128)S(1)} %copy-done, f32[64,1024]{1,0:T(8,128)S(1)} %get-tuple-element.36, f32[64]{0:T(128)S(1)} %get-tuple-element.9, ...), kind=kOutput, calls=%fused_computation.8 | convolution fusion | flops 251985920 | bytes 2441728 | tf_op jit(solution)/shard_map/krq,kql->rl/dot_general | solution.py:41
  71.1 0.2 copy.11
  71.3 3.2 %scatter_custom_fusion.1 = f32[64,1024]{0,1:T(8,128)S(1)} fusion(s32[1024]{0:T(1024)S(1)} %get-tuple-element.11, f32[1024,64]{1,0:T(8,128)S(1)} %copy.11, f32[]{:T(128)} %constant.9.clone.1), kind=kCustom, calls=%fused_computation.28 | custom fusion | bytes 262148 | tf_op jit(solution)/shard_map/scatter | solution.py:67
  74.5 0.9 %copy.13 = f32[64,1024]{1,0:T(8,128)} copy(f32[64,1024]{0,1:T(8,128)S(1)} %scatter_custom_fusion.1) | data formatting | bytes 524288
  (62 shorter events, 0.7 us)
Async XLA Ops:
  0.6 5.0 %copy-start = (f32[5,64,1024]{2,1,0:T(8,128)S(1)}, f32[5,64,1024]{2,1,0:T(8,128)}, u32[]{:S(2)}) copy-start(f32[5,64,1024]{2,1,0:T(8,128)} %param.6) | copy-start | bytes 3932164
  6.8 5.6 %collective-permute-start.1 = (f32[5,64,64]{1,2,0:T(8,128)S(1)}, f32[5,64,64]{1,2,0:T(8,128)S(1)}, u32[]{:S(2)}, u32[]{:S(2)}) collective-permute-start(f32[5,64,64]{1,2,0:T(8,128)S(1)} %convolution_bitcast_fusion.3), channel_id=1, source_target_pairs={{0,1},{1,0},{2,3},{3,2},{4,5},{5,4},{6,7},{7,6},{8,9},{9,8},{10,11... | collective-permute-start | bytes 245768 | tf_op jit(solution)/shard_map/ppermute | solution.py:15
  12.3 3.3 %collective-permute-start = (f32[2,64]{1,0:T(2,128)S(1)}, f32[2,64]{1,0:T(2,128)S(1)}, u32[]{:S(2)}, u32[]{:S(2)}) collective-permute-start(f32[2,64]{1,0:T(2,128)S(1)} %pad_maximum_fusion), channel_id=1, source_target_pairs={{0,1},{1,0},{2,3},{3,2},{4,5},{5,4},{6,7},{7,6},{8,9},{9,8},{10,11... | collective-permute-start | bytes 1544 | tf_op jit(solution)/shard_map/ppermute | solution.py:15
  12.5 6.8 %collective-permute-start.3 = (f32[4,64,64]{1,2,0:T(8,128)S(1)}, f32[4,64,64]{1,2,0:T(8,128)S(1)}, u32[]{:S(2)}, u32[]{:S(2)}) collective-permute-start(f32[4,64,64]{1,2,0:T(8,128)S(1)} %slice.131), channel_id=1, source_target_pairs={{0,2},{1,3},{2,0},{3,1},{4,6},{5,7},{6,4},{7,5},{8,10},{9,11},{10,... | collective-permute-start | bytes 196616 | tf_op jit(solution)/shard_map/ppermute | solution.py:15
  15.6 6.6 %collective-permute-start.2 = (f32[2,64]{1,0:T(2,128)S(1)}, f32[2,64]{1,0:T(2,128)S(1)}, u32[]{:S(2)}, u32[]{:S(2)}) collective-permute-start(f32[2,64]{1,0:T(2,128)S(1)} %pad_add_fusion.9), channel_id=1, source_target_pairs={{0,2},{1,3},{2,0},{3,1},{4,6},{5,7},{6,4},{7,5},{8,10},{9,11},{10,... | collective-permute-start | bytes 1544 | tf_op jit(solution)/shard_map/ppermute | solution.py:15
  19.4 7.2 %collective-permute-start.5 = (f32[3,64,64]{1,2,0:T(8,128)S(1)}, f32[3,64,64]{1,2,0:T(8,128)S(1)}, u32[]{:S(2)}, u32[]{:S(2)}) collective-permute-start(f32[3,64,64]{1,2,0:T(8,128)S(1)} %slice.134), channel_id=1, source_target_pairs={{0,4},{1,5},{2,6},{3,7},{4,0},{5,1},{6,2},{7,3},{8,12},{9,13},{10,... | collective-permute-start | bytes 147464 | tf_op jit(solution)/shard_map/ppermute | solution.py:15
  22.2 5.9 %collective-permute-start.4 = (f32[2,64]{1,0:T(2,128)S(1)}, f32[2,64]{1,0:T(2,128)S(1)}, u32[]{:S(2)}, u32[]{:S(2)}) collective-permute-start(f32[2,64]{1,0:T(2,128)S(1)} %pad_add_fusion.8), channel_id=1, source_target_pairs={{0,4},{1,5},{2,6},{3,7},{4,0},{5,1},{6,2},{7,3},{8,12},{9,13},{10,... | collective-permute-start | bytes 1544 | tf_op jit(solution)/shard_map/ppermute | solution.py:15
  26.7 4.3 %collective-permute-start.7 = (f32[2,64,64]{1,2,0:T(8,128)S(1)}, f32[2,64,64]{1,2,0:T(8,128)S(1)}, u32[]{:S(2)}, u32[]{:S(2)}) collective-permute-start(f32[2,64,64]{1,2,0:T(8,128)S(1)} %slice.137), channel_id=1, source_target_pairs={{0,8},{8,0},{16,24},{24,16},{1,9},{9,1},{17,25},{25,17},{2,10},{10... | collective-permute-start | bytes 98312 | tf_op jit(solution)/shard_map/ppermute | solution.py:15
  28.1 4.4 %collective-permute-start.6 = (f32[2,64]{1,0:T(2,128)S(1)}, f32[2,64]{1,0:T(2,128)S(1)}, u32[]{:S(2)}, u32[]{:S(2)}) collective-permute-start(f32[2,64]{1,0:T(2,128)S(1)} %pad_add_fusion.7), channel_id=1, source_target_pairs={{0,8},{8,0},{16,24},{24,16},{1,9},{9,1},{17,25},{25,17},{2,10},{10... | collective-permute-start | bytes 1544 | tf_op jit(solution)/shard_map/ppermute | solution.py:15
  31.0 4.0 %collective-permute-start.9 = (f32[1,64,64]{1,2,0:T(8,128)S(1)}, f32[1,64,64]{1,2,0:T(8,128)S(1)}, u32[]{:S(2)}, u32[]{:S(2)}) collective-permute-start(f32[1,64,64]{1,2,0:T(8,128)S(1)} %get-tuple-element.29), channel_id=1, source_target_pairs={{0,16},{8,24},{16,0},{24,8},{1,17},{9,25},{17,1},{25,9},{2,18},{10... | collective-permute-start | bytes 49160 | tf_op jit(solution)/shard_map/ppermute | solution.py:15
  32.5 3.6 %collective-permute-start.8 = (f32[2,64]{1,0:T(2,128)S(1)}, f32[2,64]{1,0:T(2,128)S(1)}, u32[]{:S(2)}, u32[]{:S(2)}) collective-permute-start(f32[2,64]{1,0:T(2,128)S(1)} %pad_add_fusion.6), channel_id=1, source_target_pairs={{0,16},{8,24},{16,0},{24,8},{1,17},{9,25},{17,1},{25,9},{2,18},{10... | collective-permute-start | bytes 1544 | tf_op jit(solution)/shard_map/ppermute | solution.py:15
  36.2 2.2 %copy-start.1 = (f32[1024,1024]{1,0:T(8,128)S(1)}, f32[1024,1024]{1,0:T(8,128)}, u32[]{:S(2)}) copy-start(f32[1024,1024]{1,0:T(8,128)} %param.5) | copy-start | bytes 12582916
  41.2 1.5 %collective-permute-start.11 = (f32[5,64,64]{1,2,0:T(8,128)S(1)}, f32[5,64,64]{1,2,0:T(8,128)S(1)}, u32[]{:S(2)}, u32[]{:S(2)}) collective-permute-start(f32[5,64,64]{1,2,0:T(8,128)S(1)} %convolution_bitcast_fusion.2), channel_id=1, source_target_pairs={{0,1},{1,0},{2,3},{3,2},{4,5},{5,4},{6,7},{7,6},{8,9},{9,8},{10,11... | collective-permute-start | bytes 245768 | tf_op jit(solution)/shard_map/ppermute | solution.py:15
  41.2 2.2 %collective-permute-start.10 = (f32[2,64]{1,0:T(2,128)S(1)}, f32[2,64]{1,0:T(2,128)S(1)}, u32[]{:S(2)}, u32[]{:S(2)}) collective-permute-start(f32[2,64]{1,0:T(2,128)S(1)} %pad_maximum_fusion.1), channel_id=1, source_target_pairs={{0,1},{1,0},{2,3},{3,2},{4,5},{5,4},{6,7},{7,6},{8,9},{9,8},{10,11... | collective-permute-start | bytes 1544 | tf_op jit(solution)/shard_map/ppermute | solution.py:15
  42.7 5.6 %collective-permute-start.13 = (f32[4,64,64]{1,2,0:T(8,128)S(1)}, f32[4,64,64]{1,2,0:T(8,128)S(1)}, u32[]{:S(2)}, u32[]{:S(2)}) collective-permute-start(f32[4,64,64]{1,2,0:T(8,128)S(1)} %slice.144), channel_id=1, source_target_pairs={{0,2},{1,3},{2,0},{3,1},{4,6},{5,7},{6,4},{7,5},{8,10},{9,11},{10,... | collective-permute-start | bytes 196616 | tf_op jit(solution)/shard_map/ppermute | solution.py:15
  43.4 7.3 %collective-permute-start.12 = (f32[2,64]{1,0:T(2,128)S(1)}, f32[2,64]{1,0:T(2,128)S(1)}, u32[]{:S(2)}, u32[]{:S(2)}) collective-permute-start(f32[2,64]{1,0:T(2,128)S(1)} %pad_add_fusion.4), channel_id=1, source_target_pairs={{0,2},{1,3},{2,0},{3,1},{4,6},{5,7},{6,4},{7,5},{8,10},{9,11},{10,... | collective-permute-start | bytes 1544 | tf_op jit(solution)/shard_map/ppermute | solution.py:15
  48.4 7.1 %collective-permute-start.15 = (f32[3,64,64]{1,2,0:T(8,128)S(1)}, f32[3,64,64]{1,2,0:T(8,128)S(1)}, u32[]{:S(2)}, u32[]{:S(2)}) collective-permute-start(f32[3,64,64]{1,2,0:T(8,128)S(1)} %slice.147), channel_id=1, source_target_pairs={{0,4},{1,5},{2,6},{3,7},{4,0},{5,1},{6,2},{7,3},{8,12},{9,13},{10,... | collective-permute-start | bytes 147464 | tf_op jit(solution)/shard_map/ppermute | solution.py:15
  50.8 6.3 %collective-permute-start.14 = (f32[2,64]{1,0:T(2,128)S(1)}, f32[2,64]{1,0:T(2,128)S(1)}, u32[]{:S(2)}, u32[]{:S(2)}) collective-permute-start(f32[2,64]{1,0:T(2,128)S(1)} %pad_add_fusion.3), channel_id=1, source_target_pairs={{0,4},{1,5},{2,6},{3,7},{4,0},{5,1},{6,2},{7,3},{8,12},{9,13},{10,... | collective-permute-start | bytes 1544 | tf_op jit(solution)/shard_map/ppermute | solution.py:15
  55.5 4.3 %collective-permute-start.17 = (f32[2,64,64]{1,2,0:T(8,128)S(1)}, f32[2,64,64]{1,2,0:T(8,128)S(1)}, u32[]{:S(2)}, u32[]{:S(2)}) collective-permute-start(f32[2,64,64]{1,2,0:T(8,128)S(1)} %slice.150), channel_id=1, source_target_pairs={{0,8},{8,0},{16,24},{24,16},{1,9},{9,1},{17,25},{25,17},{2,10},{10... | collective-permute-start | bytes 98312 | tf_op jit(solution)/shard_map/ppermute | solution.py:15
  57.1 3.6 %collective-permute-start.16 = (f32[2,64]{1,0:T(2,128)S(1)}, f32[2,64]{1,0:T(2,128)S(1)}, u32[]{:S(2)}, u32[]{:S(2)}) collective-permute-start(f32[2,64]{1,0:T(2,128)S(1)} %pad_add_fusion.2), channel_id=1, source_target_pairs={{0,8},{8,0},{16,24},{24,16},{1,9},{9,1},{17,25},{25,17},{2,10},{10... | collective-permute-start | bytes 1544 | tf_op jit(solution)/shard_map/ppermute | solution.py:15
  59.9 4.0 %collective-permute-start.19 = (f32[1,64,64]{1,2,0:T(8,128)S(1)}, f32[1,64,64]{1,2,0:T(8,128)S(1)}, u32[]{:S(2)}, u32[]{:S(2)}) collective-permute-start(f32[1,64,64]{1,2,0:T(8,128)S(1)} %get-tuple-element.25), channel_id=1, source_target_pairs={{0,16},{8,24},{16,0},{24,8},{1,17},{9,25},{17,1},{25,9},{2,18},{10... | collective-permute-start | bytes 49160 | tf_op jit(solution)/shard_map/ppermute | solution.py:15
  60.7 3.6 %collective-permute-start.18 = (f32[2,64]{1,0:T(2,128)S(1)}, f32[2,64]{1,0:T(2,128)S(1)}, u32[]{:S(2)}, u32[]{:S(2)}) collective-permute-start(f32[2,64]{1,0:T(2,128)S(1)} %pad_add_fusion.1), channel_id=1, source_target_pairs={{0,16},{8,24},{16,0},{24,8},{1,17},{9,25},{17,1},{25,9},{2,18},{10... | collective-permute-start | bytes 1544 | tf_op jit(solution)/shard_map/ppermute | solution.py:15
  63.9 0.7 copy-start.2
where the time goes:
time: 75.6 us; the launch traced here: 75.4 us
  waiting for transfers between devices  24.8 us (33%)
  starting transfers between devices  22.1 us (29%)
  local copies, waits for them, and re-layouts  13.1 us (17%)
  matrix products  13 us (17%)
  other arithmetic  1.48 us (2%)
  between operations  0.91 us (1%)
    ppermute x20, waiting for transfers between devices, swapped(): return lax.ppermute(value, axis, pairs)  24.8 us
    ppermute x20, starting transfers between devices, swapped(): return lax.ppermute(value, axis, pairs)  22.1 us
    dot_general x2, matrix products, kernel_with_sums(): jnp.dot(vector, leaf_blocks, precision=HIGH, preferred_element_type=jnp.f...  7.69 us
    scatter x1, local copies, waits for them, and re-layouts, local(): placed_sol = jnp.zeros_like(right_side).at[:, local_order].set(solution)  3.39 us
    scatter x1, local copies, waits for them, and re-layouts, local(): placed_res = jnp.zeros_like(right_side).at[:, local_order].set(residual)  3.21 us
    unnamed x9, local copies, waits for them, and re-layouts  3.1 us
    gather x2, local copies, waits for them, and re-layouts, local(): rhs_leaf = jnp.take(right_side, local_order, axis=1)  2.99 us
    dot_general x2, matrix products, kernel_with_sums(): far = jnp.einsum('krq,kql->rl', sibling, factors, precision=HIGH)  2.97 us
  transfers between devices with their start and end apart: 20, of which 11 were waited for; matrix products, arithmetic and copies ran while one was open for 7% of the time, Pallas kernels for 0%

commit v1 on v0

v1 whole, which is shorter than its diff:
```python
import jax
import jax.numpy as jnp
from jax import lax
from jax.experimental import pallas as pl
from jax.experimental.pallas import tpu as pltpu
from jax.sharding import PartitionSpec as P

AXES = ("wide", "narrow")
F32 = jnp.float32
BF16 = jnp.bfloat16
TAIL = 8
VMEM = pl.BlockSpec(memory_space=pltpu.VMEM)
HBM = pl.BlockSpec(memory_space=pltpu.HBM)


def dot(a, b):
    return jnp.dot(a, b, preferred_element_type=F32)


def dot_nt(a, b):
    return lax.dot_general(a, b, (((1,), (1,)), ((), ())), preferred_element_type=F32)


def split2(value):
    high = value.astype(BF16)
    return high, (value - high.astype(F32)).astype(BF16)


def split3(value):
    high = value.astype(BF16)
    rest = value - high.astype(F32)
    mid = rest.astype(BF16)
    return high, mid, (rest - mid.astype(F32)).astype(BF16)


def eye_mask(rows, lanes, period):
    row = lax.broadcasted_iota(jnp.int32, (rows, lanes), 0)
    lane = lax.broadcasted_iota(jnp.int32, (rows, lanes), 1)
    return (lane == row) | (lane == row + period)


def to_row(column, lanes):
    rows = column.shape[0]
    row = lax.broadcasted_iota(jnp.int32, (rows, lanes), 0)
    lane = lax.broadcasted_iota(jnp.int32, (rows, lanes), 1)
    return jnp.sum(jnp.where(row == lane, column, 0.0), axis=0, keepdims=True)


def to_column(row, rows):
    lanes = row.shape[1]
    return jnp.sum(jnp.where(eye_mask(rows, lanes, rows), row, 0.0), axis=1, keepdims=True)


def pack_projection(q_hi, q_lo, both, rhs):
    result = dot_nt(q_hi, both) + dot_nt(q_lo, both)
    full = result + pltpu.roll(result, rhs, 1)
    half = full.shape[0] // 2
    lane = lax.broadcasted_iota(jnp.int32, (half, full.shape[1]), 1)
    return jnp.where(lane < rhs, full[:half], full[half:])


def write_message(msg_ref, packed, field, near, rhs):
    lanes = 2 * rhs
    square = jnp.sum(field * field, axis=1, keepdims=True)
    product = jnp.sum(field * near, axis=1, keepdims=True)
    rows = packed.shape[0]
    msg_ref[:rows] = packed
    index = lax.broadcasted_iota(jnp.int32, (TAIL, lanes), 0)
    tail = jnp.where(index == 0, to_row(square, lanes), jnp.where(index == 1, to_row(product, lanes), 0.0))
    msg_ref[rows:] = tail


def near_product(both, field_hi, d_hi, d_lo, rhs):
    wide = dot(both, d_hi)
    return wide[:rhs] + wide[rhs:] + dot(field_hi, d_lo)


def far_product(parts, q_hi, q_lo, rhs):
    stacked = jnp.concatenate(parts, axis=0)
    turned = stacked.T
    half = q_hi.shape[0] // 2
    total = None
    for side in range(2):
        hi, lo = split2(turned[side * rhs:(side + 1) * rhs])
        both = jnp.concatenate([hi, lo], axis=0)
        wide = dot(both, q_hi[side * half:(side + 1) * half])
        part = wide[:rhs] + wide[rhs:] + dot(hi, q_lo[side * half:(side + 1) * half])
        total = part if total is None else total + part
    return total


def first_kernel(order_ref, rs_ref, d_hbm, f_hbm, b_ref, near_ref, msg_ref, dhi_ref, dlo_ref, qhi_ref, qlo_ref,
                 d_ref, f_ref, sems):
    levels, rank, leaf = f_ref.shape
    rhs = rs_ref.shape[0]
    half = rank // 2
    chunk = 256
    chunks = leaf // chunk
    f_copy = pltpu.make_async_copy(f_hbm, f_ref, sems.at[chunks])
    f_copy.start()
    d_copies = []
    for n in range(chunks):
        cols = pl.ds(n * chunk, chunk)
        copy = pltpu.make_async_copy(d_hbm.at[:, cols], d_ref.at[:, cols], sems.at[n])
        copy.start()
        d_copies.append(copy)
    hi, mid, lo = split3(rs_ref[...])
    three = jnp.concatenate([hi, mid, lo], axis=0)
    for n in range(chunks):
        cols = pl.ds(n * chunk, chunk)
        index = lax.broadcasted_iota(jnp.int32, (leaf, chunk), 0)
        onehot = jnp.where(index == order_ref[:, cols], 1.0, 0.0).astype(BF16)
        got = dot(three, onehot)
        b_ref[:, cols] = got[:rhs] + got[rhs:2 * rhs] + got[2 * rhs:]
    field = b_ref[...]
    field_hi, field_lo = split2(field)
    both = jnp.concatenate([field_hi, field_lo], axis=0)
    f_copy.wait()
    for level in range(levels):
        for side in range(2):
            hi, lo = split2(f_ref[level, pl.ds(side * half, half)])
            rows = pl.ds((side * levels + level) * half, half)
            qhi_ref[rows] = hi
            qlo_ref[rows] = lo
    packed = pack_projection(qhi_ref[...], qlo_ref[...], both, rhs)
    for n in range(chunks):
        cols = pl.ds(n * chunk, chunk)
        d_copies[n].wait()
        d_hi, d_lo = split2(d_ref[:, cols])
        dhi_ref[:, cols] = d_hi
        dlo_ref[:, cols] = d_lo
        near_ref[:, cols] = near_product(both, field_hi, d_hi, d_lo, rhs)
    write_message(msg_ref, packed, field, near_ref[...], rhs)


def second_kernel(tail_ref, *refs):
    levels = len(refs) - 10
    parts = refs[:levels]
    b_ref, near_ref, dhi_ref, dlo_ref, qhi_ref, qlo_ref = refs[levels:levels + 6]
    r_ref, image_ref, next_ref, msg_ref = refs[levels + 6:]
    rhs = b_ref.shape[0]
    half = qhi_ref.shape[0] // levels // 2
    norm = to_column(tail_ref[0:1], rhs)
    product = to_column(tail_ref[1:2], rhs)
    alpha = norm / product
    far = far_product([part[:half] for part in parts], qhi_ref[...], qlo_ref[...], rhs)
    image = near_ref[...] + far
    image_ref[...] = image
    field = b_ref[...] - alpha * image
    r_ref[...] = field
    field_hi, field_lo = split2(field)
    both = jnp.concatenate([field_hi, field_lo], axis=0)
    packed = pack_projection(qhi_ref[...], qlo_ref[...], both, rhs)
    near = near_product(both, field_hi, dhi_ref[...], dlo_ref[...], rhs)
    next_ref[...] = near
    write_message(msg_ref, packed, field, near, rhs)


def third_kernel(order_ref, old_ref, tail_ref, *refs):
    levels = len(refs) - 8
    parts = refs[:levels]
    b_ref, image_ref, r_ref, near_ref, qhi_ref, qlo_ref, x_out, r_out = refs[levels:]
    rhs, leaf = b_ref.shape
    half = qhi_ref.shape[0] // levels // 2
    norm_old = to_column(old_ref[0:1], rhs)
    alpha_old = norm_old / to_column(old_ref[1:2], rhs)
    norm = to_column(tail_ref[0:1], rhs)
    product = to_column(tail_ref[1:2], rhs)
    ratio = norm / norm_old
    alpha = norm / (product - ratio * norm / alpha_old)
    far = far_product([part[:half] for part in parts], qhi_ref[...], qlo_ref[...], rhs)
    direction = r_ref[...] + ratio * b_ref[...]
    along = near_ref[...] + far + ratio * image_ref[...]
    x = alpha_old * b_ref[...] + alpha * direction
    r = r_ref[...] - alpha * along
    three = jnp.concatenate(split3(x) + split3(r), axis=0)
    chunk = 256
    for n in range(leaf // chunk):
        cols = pl.ds(n * chunk, chunk)
        index = lax.broadcasted_iota(jnp.int32, (chunk, leaf), 0) + n * chunk
        onehot = jnp.where(index == order_ref[...], 1.0, 0.0).astype(BF16)
        got = dot_nt(three, onehot)
        x_out[:, cols] = got[:rhs] + got[rhs:2 * rhs] + got[2 * rhs:3 * rhs]
        r_out[:, cols] = got[3 * rhs:4 * rhs] + got[4 * rhs:5 * rhs] + got[5 * rhs:]


def swapped(value, level):
    mask = 2**level + (1 if level else 0)
    count = lax.axis_size("wide") * lax.axis_size("narrow")
    return lax.ppermute(value, AXES, [(source, source ^ mask) for source in range(count)])


def butterfly(message, levels, half):
    parts = []
    for level in range(levels):
        other = swapped(message, level)
        parts.append(other)
        cross = 2.0 * jnp.sum(message[:half] * other[:half], axis=0, keepdims=True)
        merged = message[half:] + other[half:]
        message = merged + jnp.pad(cross, ((merged.shape[0] - TAIL + 1, TAIL - 2), (0, 0)))
    return parts, message


def local(right_side, leaf_blocks, factors, leaf_order):
    leaf = leaf_blocks.shape[1]
    levels, rank, _ = factors.shape
    rhs = right_side.shape[0]
    half = rank // 2
    order = lax.rem(leaf_order, leaf).reshape(1, leaf)
    field = jax.ShapeDtypeStruct((rhs, leaf), F32)
    message = jax.ShapeDtypeStruct((levels * half + TAIL, 2 * rhs), F32)
    matrix = jax.ShapeDtypeStruct((leaf, leaf), BF16)
    basis = jax.ShapeDtypeStruct((levels * rank, leaf), BF16)
    params = pltpu.CompilerParams(vmem_limit_bytes=32 * 1024 * 1024)
    chunks = leaf // 256
    b, near, msg, dhi, dlo, qhi, qlo = pl.pallas_call(
        first_kernel,
        out_shape=(field, field, message, matrix, matrix, basis, basis),
        in_specs=[VMEM, VMEM, HBM, HBM],
        out_specs=(VMEM,) * 7,
        scratch_shapes=[
            pltpu.VMEM((leaf, leaf), F32),
            pltpu.VMEM(factors.shape, F32),
            pltpu.SemaphoreType.DMA((chunks + 1,)),
        ],
        compiler_params=params,
        name="first",
    )(order, right_side, leaf_blocks, factors)
    parts, tail = butterfly(msg, levels, half)
    r, image, near_next, msg = pl.pallas_call(
        second_kernel,
        out_shape=(field, field, field, message),
        in_specs=[VMEM] * (7 + levels),
        out_specs=(VMEM,) * 4,
        compiler_params=params,
        name="second",
    )(tail, *parts, b, near, dhi, dlo, qhi, qlo)
    parts, tail_next = butterfly(msg, levels, half)
    return pl.pallas_call(
        third_kernel,
        out_shape=(field, field),
        in_specs=[VMEM] * (9 + levels),
        out_specs=(VMEM,) * 2,
        compiler_params=params,
        name="third",
    )(order, tail, tail_next, *parts, b, image, r, near_next, qhi, qlo)


def solution(mesh):
    placed = (
        P(None, AXES),
        P(AXES, None),
        P(None, None, AXES),
        P(AXES),
    )
    return jax.shard_map(
        local,
        mesh=mesh,
        in_specs=placed,
        out_specs=(P(None, AXES), P(None, AXES)),
        check_vma=False,
    )
```

time: 75.6 us -> 51.3 us (0.68)
  matrix products: 13 us -> 0 us
  local copies, waits for them, and re-layouts: 13.1 us -> 4.45 us
  Pallas kernels: 0 us -> 8.19 us
  waiting for transfers between devices: 24.8 us -> 19 us
  starting transfers between devices: 22.1 us -> 17.5 us
    dot_general x6 -> x0, matrix products: 13 us -> none  [the longest x2 7.69 us: kernel_with_sums(): jnp.dot(vector, leaf_blocks, precision=HIGH, preferred_element_type=jnp.f...]
    pallas_call x0 -> x3, Pallas kernels: none -> 8.19 us  [the longest x1 4.25 us: local(): pl.pallas_call(first_kernel, out_shape=(field, field, message, matrix, ma...]
    scatter x2 -> x0, local copies, waits for them, and re-layouts: 6.61 us -> none  [the longest x1 3.39 us: local(): placed_sol = jnp.zeros_like(right_side).at[:, local_order].set(solution)]
    ppermute x20 -> x10, waiting for transfers between devices: 24.8 us -> 19 us  [swapped(): lax.ppermute(value, AXES, [(source, source ^ mask) for source in range(co...]
    ppermute x20 -> x10, starting transfers between devices: 22.1 us -> 17.5 us  [swapped(): lax.ppermute(value, AXES, [(source, source ^ mask) for source in range(co...]
    gather x2 -> x0, local copies, waits for them, and re-layouts: 2.99 us -> none  [local(): rhs_leaf = jnp.take(right_side, local_order, axis=1)]
    unnamed x9 -> x6, local copies, waits for them, and re-layouts: 3.1 us -> 4.45 us
    and x1 -> x0, other arithmetic: 0.8 us -> none  [local(): rhs_leaf = jnp.take(right_side, local_order, axis=1)]
  transfers between devices with their start and end apart: 20 -> 10, of which waited for: 11 -> 10; matrix products, arithmetic and copies ran while one was open for 7% -> 0% of each run, Pallas kernels for 0% -> 0%
where the time goes in v1:
time: 51.3 us; the launch traced here: 50.9 us
  waiting for transfers between devices  19 us (37%)
  starting transfers between devices  17.5 us (34%)
  Pallas kernels  8.19 us (16%)
  local copies, waits for them, and re-layouts  4.45 us (9%)
  other arithmetic  1.09 us (2%)
  between operations  0.69 us (1%)
    ppermute x10, waiting for transfers between devices, swapped(): lax.ppermute(value, AXES, [(source, source ^ mask) for source in range(co...  19 us
    ppermute x10, starting transfers between devices, swapped(): lax.ppermute(value, AXES, [(source, source ^ mask) for source in range(co...  17.5 us
    unnamed x6, local copies, waits for them, and re-layouts  4.45 us
    pallas_call x1, Pallas kernels, local(): pl.pallas_call(first_kernel, out_shape=(field, field, message, matrix, ma...  4.25 us
    pallas_call x1, Pallas kernels, local(): pl.pallas_call(third_kernel, out_shape=(field, field), in_specs=[VMEM] *...  2.13 us
    pallas_call x1, Pallas kernels, local(): pl.pallas_call(second_kernel, out_shape=(field, field, field, message), i...  1.81 us
  transfers between devices with their start and end apart: 10, of which 10 were waited for; matrix products, arithmetic and copies ran while one was open for 0% of the time, Pallas kernels for 0%

profile of v1, /device:TPU:0, one launch (start us, length us, event | category | flops | bytes accessed | tf_op | source)
XLA Modules:
  0.0 50.9 jit_solution(9545617940785460078)
XLA Ops:
  0.6 0.7 %negate_select_fusion = s32[1024]{0:T(1024)S(1)} fusion(s32[1024]{0:T(1024)} %param.7), kind=kLoop, calls=%fused_computation.36 | loop fusion | flops 6144 | bytes 8192 | tf_op jit(solution)/shard_map/rem | solution.py:209
  1.3 0.0 copy-start
  1.3 2.2 %copy-done = f32[1024,1024]{1,0:T(8,128)S(1)} copy-done((f32[1024,1024]{1,0:T(8,128)S(1)}, f32[1024,1024]{1,0:T(8,128)}, u32[]{:S(2)}) %copy-start) | copy-done | bytes 4194328
  3.5 0.0 copy-start.1
  3.5 1.3 %copy-done.1 = f32[5,64,1024]{2,1,0:T(8,128)S(1)} copy-done((f32[5,64,1024]{2,1,0:T(8,128)S(1)}, f32[5,64,1024]{2,1,0:T(8,128)}, u32[]{:S(2)}) %copy-start.1) | copy-done | bytes 1310744
  4.8 0.0 copy-start.2
  4.8 0.9 %copy-done.2 = f32[64,1024]{1,0:T(8,128)S(1)} copy-done((f32[64,1024]{1,0:T(8,128)S(1)}, f32[64,1024]{1,0:T(8,128)}, u32[]{:S(2)}) %copy-start.2) | copy-done | bytes 262168
  5.8 4.2 %first.1 = (f32[64,1024]{1,0:T(8,128)S(1)}, f32[64,1024]{1,0:T(8,128)S(1)}, f32[168,128]{1,0:T(8,128)S(1)}, bf16[1024,1024]{1,0:T(8,128)(2,1)S(1)}, bf16[1024,10...) custom-call(s32[1,1024]{1,0:T(1,128)S(1)} %bitcast.21, f32[64,1024]{1,0:T(8,128)S(1)} %copy-done.2, ...), custom_call_target="tpu_custom_call" | custom-call | tf_op jit(solution)/shard_map/first/pallas_call | solution.py:216
  10.0 0.6 %collective-permute-start = (f32[168,128]{1,0:T(8,128)S(1)}, f32[168,128]{1,0:T(8,128)S(1)}, u32[]{:S(2)}, u32[]{:S(2)}) collective-permute-start(f32[168,128]{1,0:T(8,128)S(1)} %get-tuple-element.13), channel_id=1, source_target_pairs={{0,1},{1,0},{2,3},{3,2},{4,5},{5,4},{6,7},{7,6},{8,9},{9,8},{10,11... | collective-permute-start | bytes 258056 | tf_op jit(solution)/shard_map/ppermute | solution.py:190
  10.6 0.9 %collective-permute-done.refs_0_ = f32[168,128]{1,0:T(8,128)S(1)} collective-permute-done((f32[168,128]{1,0:T(8,128)S(1)}, f32[168,128]{1,0:T(8,128)S(1)}, u32[]{:S(2)}, u32[]{:S(2)}) %collective-permute-start) | collective-permute-done | bytes 86048 | tf_op jit(solution)/shard_map/ppermute | solution.py:190
  11.6 2.7 %collective-permute-start.1 = (f32[136,128]{1,0:T(8,128)S(1)}, f32[136,128]{1,0:T(8,128)S(1)}, u32[]{:S(2)}, u32[]{:S(2)}) collective-permute-start(f32[136,128]{1,0:T(8,128)S(1)} %fusion.1), channel_id=1, source_target_pairs={{0,3},{1,2},{2,1},{3,0},{4,7},{5,6},{6,5},{7,4},{8,11},{9,10},{10,... | collective-permute-start | bytes 208904 | tf_op jit(solution)/shard_map/ppermute | solution.py:190
  14.3 2.2 %collective-permute-done.1.refs_1_ = f32[136,128]{1,0:T(8,128)S(1)} collective-permute-done((f32[136,128]{1,0:T(8,128)S(1)}, f32[136,128]{1,0:T(8,128)S(1)}, u32[]{:S(2)}, u32[]{:S(2)}) %collective-permute-start.1) | collective-permute-done | bytes 69664 | tf_op jit(solution)/shard_map/ppermute | solution.py:190
  16.6 3.0 %collective-permute-start.2 = (f32[104,128]{1,0:T(8,128)S(1)}, f32[104,128]{1,0:T(8,128)S(1)}, u32[]{:S(2)}, u32[]{:S(2)}) collective-permute-start(f32[104,128]{1,0:T(8,128)S(1)} %fusion.3), channel_id=1, source_target_pairs={{0,5},{1,4},{2,7},{3,6},{4,1},{5,0},{6,3},{7,2},{8,13},{9,12},{10,... | collective-permute-start | bytes 159752 | tf_op jit(solution)/shard_map/ppermute | solution.py:190
  19.6 1.9 %collective-permute-done.2.refs_2_ = f32[104,128]{1,0:T(8,128)S(1)} collective-permute-done((f32[104,128]{1,0:T(8,128)S(1)}, f32[104,128]{1,0:T(8,128)S(1)}, u32[]{:S(2)}, u32[]{:S(2)}) %collective-permute-start.2) | collective-permute-done | bytes 53280 | tf_op jit(solution)/shard_map/ppermute | solution.py:190
  21.5 2.9 %collective-permute-start.3 = (f32[72,128]{1,0:T(8,128)S(1)}, f32[72,128]{1,0:T(8,128)S(1)}, u32[]{:S(2)}, u32[]{:S(2)}) collective-permute-start(f32[72,128]{1,0:T(8,128)S(1)} %fusion.5), channel_id=1, source_target_pairs={{0,9},{1,8},{2,11},{3,10},{4,13},{5,12},{6,15},{7,14},{8,1},{9,0},... | collective-permute-start | bytes 110600 | tf_op jit(solution)/shard_map/ppermute | solution.py:190
  24.4 1.6 %collective-permute-done.3.refs_3_ = f32[72,128]{1,0:T(8,128)S(1)} collective-permute-done((f32[72,128]{1,0:T(8,128)S(1)}, f32[72,128]{1,0:T(8,128)S(1)}, u32[]{:S(2)}, u32[]{:S(2)}) %collective-permute-start.3) | collective-permute-done | bytes 36896 | tf_op jit(solution)/shard_map/ppermute | solution.py:190
  26.1 1.8 %collective-permute-start.4 = (f32[40,128]{1,0:T(8,128)S(1)}, f32[40,128]{1,0:T(8,128)S(1)}, u32[]{:S(2)}, u32[]{:S(2)}) collective-permute-start(f32[40,128]{1,0:T(8,128)S(1)} %fusion.7), channel_id=1, source_target_pairs={{0,17},{1,16},{2,19},{3,18},{4,21},{5,20},{6,23},{7,22},{8,25},{9,... | collective-permute-start | bytes 61448 | tf_op jit(solution)/shard_map/ppermute | solution.py:190
  27.9 1.6 %collective-permute-done.4.refs_4_ = f32[40,128]{1,0:T(8,128)S(1)} collective-permute-done((f32[40,128]{1,0:T(8,128)S(1)}, f32[40,128]{1,0:T(8,128)S(1)}, u32[]{:S(2)}, u32[]{:S(2)}) %collective-permute-start.4) | collective-permute-done | bytes 20512 | tf_op jit(solution)/shard_map/ppermute | solution.py:190
  29.6 1.8 %second.1 = (f32[64,1024]{1,0:T(8,128)S(1)}, f32[64,1024]{1,0:T(8,128)S(1)}, f32[64,1024]{1,0:T(8,128)S(1)}, f32[168,128]{1,0:T(8,128)S(1)}) custom-call(f32[8,128]{1,0:T(8,128)S(1)} %fusion.20.tail_ref.old_ref, f32[168,128]{1,0:T(8,128)S(1)} %collective-permute-done.refs_0_, f32[136,128]{1,0:T(8,128)S(1)} %collective-permute-done.1.refs_1_, ...), custom_call_target="tpu_custom_call" | custom-call | tf_op jit(solution)/shard_map/second/pallas_call | solution.py:230
  31.4 0.2 collective-permute-start.5
  31.6 1.2 %collective-permute-done.5.refs_0_ = f32[168,128]{1,0:T(8,128)S(1)} collective-permute-done((f32[168,128]{1,0:T(8,128)S(1)}, f32[168,128]{1,0:T(8,128)S(1)}, u32[]{:S(2)}, u32[]{:S(2)}) %collective-permute-start.5) | collective-permute-done | bytes 86048 | tf_op jit(solution)/shard_map/ppermute | solution.py:190
  32.8 1.3 %collective-permute-start.6 = (f32[136,128]{1,0:T(8,128)S(1)}, f32[136,128]{1,0:T(8,128)S(1)}, u32[]{:S(2)}, u32[]{:S(2)}) collective-permute-start(f32[136,128]{1,0:T(8,128)S(1)} %fusion), channel_id=1, source_target_pairs={{0,3},{1,2},{2,1},{3,0},{4,7},{5,6},{6,5},{7,4},{8,11},{9,10},{10,... | collective-permute-start | bytes 208904 | tf_op jit(solution)/shard_map/ppermute | solution.py:190
  34.1 2.9 %collective-permute-done.6.refs_1_ = f32[136,128]{1,0:T(8,128)S(1)} collective-permute-done((f32[136,128]{1,0:T(8,128)S(1)}, f32[136,128]{1,0:T(8,128)S(1)}, u32[]{:S(2)}, u32[]{:S(2)}) %collective-permute-start.6) | collective-permute-done | bytes 69664 | tf_op jit(solution)/shard_map/ppermute | solution.py:190
  37.1 2.6 %collective-permute-start.7 = (f32[104,128]{1,0:T(8,128)S(1)}, f32[104,128]{1,0:T(8,128)S(1)}, u32[]{:S(2)}, u32[]{:S(2)}) collective-permute-start(f32[104,128]{1,0:T(8,128)S(1)} %fusion.2), channel_id=1, source_target_pairs={{0,5},{1,4},{2,7},{3,6},{4,1},{5,0},{6,3},{7,2},{8,13},{9,12},{10,... | collective-permute-start | bytes 159752 | tf_op jit(solution)/shard_map/ppermute | solution.py:190
  39.7 2.2 %collective-permute-done.7.refs_2_ = f32[104,128]{1,0:T(8,128)S(1)} collective-permute-done((f32[104,128]{1,0:T(8,128)S(1)}, f32[104,128]{1,0:T(8,128)S(1)}, u32[]{:S(2)}, u32[]{:S(2)}) %collective-permute-start.7) | collective-permute-done | bytes 53280 | tf_op jit(solution)/shard_map/ppermute | solution.py:190
  41.9 1.2 %collective-permute-start.8 = (f32[72,128]{1,0:T(8,128)S(1)}, f32[72,128]{1,0:T(8,128)S(1)}, u32[]{:S(2)}, u32[]{:S(2)}) collective-permute-start(f32[72,128]{1,0:T(8,128)S(1)} %fusion.4), channel_id=1, source_target_pairs={{0,9},{1,8},{2,11},{3,10},{4,13},{5,12},{6,15},{7,14},{8,1},{9,0},... | collective-permute-start | bytes 110600 | tf_op jit(solution)/shard_map/ppermute | solution.py:190
  43.1 2.3 %collective-permute-done.8.refs_3_ = f32[72,128]{1,0:T(8,128)S(1)} collective-permute-done((f32[72,128]{1,0:T(8,128)S(1)}, f32[72,128]{1,0:T(8,128)S(1)}, u32[]{:S(2)}, u32[]{:S(2)}) %collective-permute-start.8) | collective-permute-done | bytes 36896 | tf_op jit(solution)/shard_map/ppermute | solution.py:190
  45.4 1.2 %collective-permute-start.9 = (f32[40,128]{1,0:T(8,128)S(1)}, f32[40,128]{1,0:T(8,128)S(1)}, u32[]{:S(2)}, u32[]{:S(2)}) collective-permute-start(f32[40,128]{1,0:T(8,128)S(1)} %fusion.6), channel_id=1, source_target_pairs={{0,17},{1,16},{2,19},{3,18},{4,21},{5,20},{6,23},{7,22},{8,25},{9,... | collective-permute-start | bytes 61448 | tf_op jit(solution)/shard_map/ppermute | solution.py:190
  46.6 2.1 %collective-permute-done.9.refs_4_ = f32[40,128]{1,0:T(8,128)S(1)} collective-permute-done((f32[40,128]{1,0:T(8,128)S(1)}, f32[40,128]{1,0:T(8,128)S(1)}, u32[]{:S(2)}, u32[]{:S(2)}) %collective-permute-start.9) | collective-permute-done | bytes 20512 | tf_op jit(solution)/shard_map/ppermute | solution.py:190
  48.7 2.1 %third.1 = (f32[64,1024]{1,0:T(8,128)}, f32[64,1024]{1,0:T(8,128)}) custom-call(s32[1,1024]{1,0:T(1,128)S(1)} %bitcast.22, f32[8,128]{1,0:T(8,128)S(1)} %fusion.20.tail_ref.old_ref, f32[8,128]{1,0:T(8,128)S(1)} %fusion.19.tail_ref, f32[168,128]{1,0:T(8,128)S(1)} %collective-permute-done.5.refs_0_, f32[136,128]{1,0:T(8,128)S(1)} %collective-permute-done.6.refs_1_, ...), custom_call_target="tpu_custom_call" | custom-call | tf_op jit(solution)/shard_map/third/pallas_call | solution.py:239
  (30 shorter events, 0.4 us)
Async XLA Ops:
  1.3 2.2 %copy-start = (f32[1024,1024]{1,0:T(8,128)S(1)}, f32[1024,1024]{1,0:T(8,128)}, u32[]{:S(2)}) copy-start(f32[1024,1024]{1,0:T(8,128)} %d_hbm.1) | copy-start | bytes 12582916
  3.5 1.3 %copy-start.1 = (f32[5,64,1024]{2,1,0:T(8,128)S(1)}, f32[5,64,1024]{2,1,0:T(8,128)}, u32[]{:S(2)}) copy-start(f32[5,64,1024]{2,1,0:T(8,128)} %f_hbm.1) | copy-start | bytes 3932164
  4.8 0.9 %copy-start.2 = (f32[64,1024]{1,0:T(8,128)S(1)}, f32[64,1024]{1,0:T(8,128)}, u32[]{:S(2)}) copy-start(f32[64,1024]{1,0:T(8,128)} %rs_ref.1) | copy-start | bytes 786436
  10.0 1.5 %collective-permute-start = (f32[168,128]{1,0:T(8,128)S(1)}, f32[168,128]{1,0:T(8,128)S(1)}, u32[]{:S(2)}, u32[]{:S(2)}) collective-permute-start(f32[168,128]{1,0:T(8,128)S(1)} %get-tuple-element.13), channel_id=1, source_target_pairs={{0,1},{1,0},{2,3},{3,2},{4,5},{5,4},{6,7},{7,6},{8,9},{9,8},{10,11... | collective-permute-start | bytes 258056 | tf_op jit(solution)/shard_map/ppermute | solution.py:190
  11.6 5.0 %collective-permute-start.1 = (f32[136,128]{1,0:T(8,128)S(1)}, f32[136,128]{1,0:T(8,128)S(1)}, u32[]{:S(2)}, u32[]{:S(2)}) collective-permute-start(f32[136,128]{1,0:T(8,128)S(1)} %fusion.1), channel_id=1, source_target_pairs={{0,3},{1,2},{2,1},{3,0},{4,7},{5,6},{6,5},{7,4},{8,11},{9,10},{10,... | collective-permute-start | bytes 208904 | tf_op jit(solution)/shard_map/ppermute | solution.py:190
  16.6 4.9 %collective-permute-start.2 = (f32[104,128]{1,0:T(8,128)S(1)}, f32[104,128]{1,0:T(8,128)S(1)}, u32[]{:S(2)}, u32[]{:S(2)}) collective-permute-start(f32[104,128]{1,0:T(8,128)S(1)} %fusion.3), channel_id=1, source_target_pairs={{0,5},{1,4},{2,7},{3,6},{4,1},{5,0},{6,3},{7,2},{8,13},{9,12},{10,... | collective-permute-start | bytes 159752 | tf_op jit(solution)/shard_map/ppermute | solution.py:190
  21.5 4.6 %collective-permute-start.3 = (f32[72,128]{1,0:T(8,128)S(1)}, f32[72,128]{1,0:T(8,128)S(1)}, u32[]{:S(2)}, u32[]{:S(2)}) collective-permute-start(f32[72,128]{1,0:T(8,128)S(1)} %fusion.5), channel_id=1, source_target_pairs={{0,9},{1,8},{2,11},{3,10},{4,13},{5,12},{6,15},{7,14},{8,1},{9,0},... | collective-permute-start | bytes 110600 | tf_op jit(solution)/shard_map/ppermute | solution.py:190
  26.1 3.5 %collective-permute-start.4 = (f32[40,128]{1,0:T(8,128)S(1)}, f32[40,128]{1,0:T(8,128)S(1)}, u32[]{:S(2)}, u32[]{:S(2)}) collective-permute-start(f32[40,128]{1,0:T(8,128)S(1)} %fusion.7), channel_id=1, source_target_pairs={{0,17},{1,16},{2,19},{3,18},{4,21},{5,20},{6,23},{7,22},{8,25},{9,... | collective-permute-start | bytes 61448 | tf_op jit(solution)/shard_map/ppermute | solution.py:190
  31.4 1.3 %collective-permute-start.5 = (f32[168,128]{1,0:T(8,128)S(1)}, f32[168,128]{1,0:T(8,128)S(1)}, u32[]{:S(2)}, u32[]{:S(2)}) collective-permute-start(f32[168,128]{1,0:T(8,128)S(1)} %get-tuple-element.20), channel_id=1, source_target_pairs={{0,1},{1,0},{2,3},{3,2},{4,5},{5,4},{6,7},{7,6},{8,9},{9,8},{10,11... | collective-permute-start | bytes 258056 | tf_op jit(solution)/shard_map/ppermute | solution.py:190
  32.8 4.2 %collective-permute-start.6 = (f32[136,128]{1,0:T(8,128)S(1)}, f32[136,128]{1,0:T(8,128)S(1)}, u32[]{:S(2)}, u32[]{:S(2)}) collective-permute-start(f32[136,128]{1,0:T(8,128)S(1)} %fusion), channel_id=1, source_target_pairs={{0,3},{1,2},{2,1},{3,0},{4,7},{5,6},{6,5},{7,4},{8,11},{9,10},{10,... | collective-permute-start | bytes 208904 | tf_op jit(solution)/shard_map/ppermute | solution.py:190
  37.1 4.8 %collective-permute-start.7 = (f32[104,128]{1,0:T(8,128)S(1)}, f32[104,128]{1,0:T(8,128)S(1)}, u32[]{:S(2)}, u32[]{:S(2)}) collective-permute-start(f32[104,128]{1,0:T(8,128)S(1)} %fusion.2), channel_id=1, source_target_pairs={{0,5},{1,4},{2,7},{3,6},{4,1},{5,0},{6,3},{7,2},{8,13},{9,12},{10,... | collective-permute-start | bytes 159752 | tf_op jit(solution)/shard_map/ppermute | solution.py:190
  41.9 3.5 %collective-permute-start.8 = (f32[72,128]{1,0:T(8,128)S(1)}, f32[72,128]{1,0:T(8,128)S(1)}, u32[]{:S(2)}, u32[]{:S(2)}) collective-permute-start(f32[72,128]{1,0:T(8,128)S(1)} %fusion.4), channel_id=1, source_target_pairs={{0,9},{1,8},{2,11},{3,10},{4,13},{5,12},{6,15},{7,14},{8,1},{9,0},... | collective-permute-start | bytes 110600 | tf_op jit(solution)/shard_map/ppermute | solution.py:190
  45.4 3.3 %collective-permute-start.9 = (f32[40,128]{1,0:T(8,128)S(1)}, f32[40,128]{1,0:T(8,128)S(1)}, u32[]{:S(2)}, u32[]{:S(2)}) collective-permute-start(f32[40,128]{1,0:T(8,128)S(1)} %fusion.6), channel_id=1, source_target_pairs={{0,17},{1,16},{2,19},{3,18},{4,21},{5,20},{6,23},{7,22},{8,25},{9,... | collective-permute-start | bytes 61448 | tf_op jit(solution)/shard_map/ppermute | solution.py:190

commit v2 on v1

--- a/solution.py
+++ b/solution.py
@@ -89,13 +89,17 @@
     return total
 
 
-def first_kernel(order_ref, rs_ref, d_hbm, f_hbm, b_ref, near_ref, msg_ref, dhi_ref, dlo_ref, qhi_ref, qlo_ref,
-                 d_ref, f_ref, sems):
+def first_kernel(order_hbm, rs_hbm, d_hbm, f_hbm, b_ref, near_ref, msg_ref, dhi_ref, dlo_ref, qhi_ref, qlo_ref, order_ref,
+                 rs_ref, d_ref, f_ref, sems):
     levels, rank, leaf = f_ref.shape
     rhs = rs_ref.shape[0]
     half = rank // 2
     chunk = 256
     chunks = leaf // chunk
+    order_copy = pltpu.make_async_copy(order_hbm, order_ref, sems.at[chunks + 1])
+    order_copy.start()
+    rs_copy = pltpu.make_async_copy(rs_hbm, rs_ref, sems.at[chunks + 2])
+    rs_copy.start()
     f_copy = pltpu.make_async_copy(f_hbm, f_ref, sems.at[chunks])
     f_copy.start()
     d_copies = []
@@ -104,12 +108,15 @@
         copy = pltpu.make_async_copy(d_hbm.at[:, cols], d_ref.at[:, cols], sems.at[n])
         copy.start()
         d_copies.append(copy)
+    order_copy.wait()
+    rs_copy.wait()
     hi, mid, lo = split3(rs_ref[...])
     three = jnp.concatenate([hi, mid, lo], axis=0)
     for n in range(chunks):
         cols = pl.ds(n * chunk, chunk)
         index = lax.broadcasted_iota(jnp.int32, (leaf, chunk), 0)
-        onehot = jnp.where(index == order_ref[:, cols], 1.0, 0.0).astype(BF16)
+        local_order = lax.rem(order_ref[:, cols], leaf)
+        onehot = jnp.where(index == local_order, 1.0, 0.0).astype(BF16)
         got = dot(three, onehot)
         b_ref[:, cols] = got[:rhs] + got[rhs:2 * rhs] + got[2 * rhs:]
     field = b_ref[...]
@@ -175,10 +182,11 @@
     r = r_ref[...] - alpha * along
     three = jnp.concatenate(split3(x) + split3(r), axis=0)
     chunk = 256
+    local_order = lax.rem(order_ref[...], leaf)
     for n in range(leaf // chunk):
         cols = pl.ds(n * chunk, chunk)
         index = lax.broadcasted_iota(jnp.int32, (chunk, leaf), 0) + n * chunk
-        onehot = jnp.where(index == order_ref[...], 1.0, 0.0).astype(BF16)
+        onehot = jnp.where(index == local_order, 1.0, 0.0).astype(BF16)
         got = dot_nt(three, onehot)
         x_out[:, cols] = got[:rhs] + got[rhs:2 * rhs] + got[2 * rhs:3 * rhs]
         r_out[:, cols] = got[3 * rhs:4 * rhs] + got[4 * rhs:5 * rhs] + got[5 * rhs:]
@@ -206,26 +214,28 @@
     levels, rank, _ = factors.shape
     rhs = right_side.shape[0]
     half = rank // 2
-    order = lax.rem(leaf_order, leaf).reshape(1, leaf)
+    order = leaf_order.reshape(1, leaf)
+    hbm = [pltpu.with_memory_space_constraint(value, pltpu.HBM) for value in (order, right_side, leaf_blocks, factors)]
     field = jax.ShapeDtypeStruct((rhs, leaf), F32)
     message = jax.ShapeDtypeStruct((levels * half + TAIL, 2 * rhs), F32)
     matrix = jax.ShapeDtypeStruct((leaf, leaf), BF16)
     basis = jax.ShapeDtypeStruct((levels * rank, leaf), BF16)
     params = pltpu.CompilerParams(vmem_limit_bytes=32 * 1024 * 1024)
     chunks = leaf // 256
-    b, near, msg, dhi, dlo, qhi, qlo = pl.pallas_call(
+    b, near, msg, dhi, dlo, qhi, qlo, order = pl.pallas_call(
         first_kernel,
-        out_shape=(field, field, message, matrix, matrix, basis, basis),
-        in_specs=[VMEM, VMEM, HBM, HBM],
-        out_specs=(VMEM,) * 7,
+        out_shape=(field, field, message, matrix, matrix, basis, basis, jax.ShapeDtypeStruct((1, leaf), jnp.int32)),
+        in_specs=[HBM] * 4,
+        out_specs=(VMEM,) * 8,
         scratch_shapes=[
+            pltpu.VMEM((rhs, leaf), F32),
             pltpu.VMEM((leaf, leaf), F32),
             pltpu.VMEM(factors.shape, F32),
-            pltpu.SemaphoreType.DMA((chunks + 1,)),
+            pltpu.SemaphoreType.DMA((chunks + 3,)),
         ],
         compiler_params=params,
         name="first",
-    )(order, right_side, leaf_blocks, factors)
+    )(*hbm)
     parts, tail = butterfly(msg, levels, half)
     r, image, near_next, msg = pl.pallas_call(
         second_kernel,

time: 51.3 us -> 46.4 us (0.904)
  local copies, waits for them, and re-layouts: 4.45 us -> 0 us
  other arithmetic: 1.09 us -> 0.39 us
    unnamed x6 -> x0, local copies, waits for them, and re-layouts: 4.45 us -> none
    rem x1 -> x0, other arithmetic: 0.69 us -> none  [local(): order = lax.rem(leaf_order, leaf).reshape(1, leaf)]
where the time goes in v2:
time: 46.4 us; the launch traced here: 46 us
  waiting for transfers between devices  18.9 us (41%)
  starting transfers between devices  17.5 us (38%)
  Pallas kernels  8.51 us (18%)
  between operations  0.68 us (1%)
    ppermute x10, waiting for transfers between devices, swapped(): lax.ppermute(value, AXES, [(source, source ^ mask) for source in range(co...  18.9 us
    ppermute x10, starting transfers between devices, swapped(): lax.ppermute(value, AXES, [(source, source ^ mask) for source in range(co...  17.5 us
    pallas_call x1, Pallas kernels, local(): pl.pallas_call(first_kernel, out_shape=(field, field, message, matrix, ma...  4.62 us
    pallas_call x1, Pallas kernels, local(): pl.pallas_call(third_kernel, out_shape=(field, field), in_specs=[VMEM] *...  2.09 us
    pallas_call x1, Pallas kernels, local(): pl.pallas_call(second_kernel, out_shape=(field, field, field, message), i...  1.8 us
  transfers between devices with their start and end apart: 10, of which 10 were waited for; matrix products, arithmetic and copies ran while one was open for 0% of the time, Pallas kernels for 0%

profile of v2, /device:TPU:0, one launch (start us, length us, event | category | flops | bytes accessed | tf_op | source)
XLA Modules:
  0.0 46.0 jit_solution(11009822767523880484)
XLA Ops:
  0.6 4.6 %first.1 = (f32[64,1024]{1,0:T(8,128)S(1)}, f32[64,1024]{1,0:T(8,128)S(1)}, f32[168,128]{1,0:T(8,128)S(1)}, bf16[1024,1024]{1,0:T(8,128)(2,1)S(1)}, bf16[1024,10...) custom-call(s32[1,1024]{1,0:T(1,128)} %bitcast.21, ...), custom_call_target="tpu_custom_call" | custom-call | tf_op jit(solution)/shard_map/first/pallas_call | solution.py:225
  5.3 0.6 %collective-permute-start = (f32[168,128]{1,0:T(8,128)S(1)}, f32[168,128]{1,0:T(8,128)S(1)}, u32[]{:S(2)}, u32[]{:S(2)}) collective-permute-start(f32[168,128]{1,0:T(8,128)S(1)} %get-tuple-element.15), channel_id=1, source_target_pairs={{0,1},{1,0},{2,3},{3,2},{4,5},{5,4},{6,7},{7,6},{8,9},{9,8},{10,11... | collective-permute-start | bytes 258056 | tf_op jit(solution)/shard_map/ppermute | solution.py:198
  5.8 0.9 %collective-permute-done.refs_0_ = f32[168,128]{1,0:T(8,128)S(1)} collective-permute-done((f32[168,128]{1,0:T(8,128)S(1)}, f32[168,128]{1,0:T(8,128)S(1)}, u32[]{:S(2)}, u32[]{:S(2)}) %collective-permute-start) | collective-permute-done | bytes 86048 | tf_op jit(solution)/shard_map/ppermute | solution.py:198
  6.8 2.7 %collective-permute-start.1 = (f32[136,128]{1,0:T(8,128)S(1)}, f32[136,128]{1,0:T(8,128)S(1)}, u32[]{:S(2)}, u32[]{:S(2)}) collective-permute-start(f32[136,128]{1,0:T(8,128)S(1)} %fusion.1), channel_id=1, source_target_pairs={{0,3},{1,2},{2,1},{3,0},{4,7},{5,6},{6,5},{7,4},{8,11},{9,10},{10,... | collective-permute-start | bytes 208904 | tf_op jit(solution)/shard_map/ppermute | solution.py:198
  9.5 2.2 %collective-permute-done.1.refs_1_ = f32[136,128]{1,0:T(8,128)S(1)} collective-permute-done((f32[136,128]{1,0:T(8,128)S(1)}, f32[136,128]{1,0:T(8,128)S(1)}, u32[]{:S(2)}, u32[]{:S(2)}) %collective-permute-start.1) | collective-permute-done | bytes 69664 | tf_op jit(solution)/shard_map/ppermute | solution.py:198
  11.8 3.0 %collective-permute-start.2 = (f32[104,128]{1,0:T(8,128)S(1)}, f32[104,128]{1,0:T(8,128)S(1)}, u32[]{:S(2)}, u32[]{:S(2)}) collective-permute-start(f32[104,128]{1,0:T(8,128)S(1)} %fusion.3), channel_id=1, source_target_pairs={{0,5},{1,4},{2,7},{3,6},{4,1},{5,0},{6,3},{7,2},{8,13},{9,12},{10,... | collective-permute-start | bytes 159752 | tf_op jit(solution)/shard_map/ppermute | solution.py:198
  14.8 1.9 %collective-permute-done.2.refs_2_ = f32[104,128]{1,0:T(8,128)S(1)} collective-permute-done((f32[104,128]{1,0:T(8,128)S(1)}, f32[104,128]{1,0:T(8,128)S(1)}, u32[]{:S(2)}, u32[]{:S(2)}) %collective-permute-start.2) | collective-permute-done | bytes 53280 | tf_op jit(solution)/shard_map/ppermute | solution.py:198
  16.7 2.9 %collective-permute-start.3 = (f32[72,128]{1,0:T(8,128)S(1)}, f32[72,128]{1,0:T(8,128)S(1)}, u32[]{:S(2)}, u32[]{:S(2)}) collective-permute-start(f32[72,128]{1,0:T(8,128)S(1)} %fusion.5), channel_id=1, source_target_pairs={{0,9},{1,8},{2,11},{3,10},{4,13},{5,12},{6,15},{7,14},{8,1},{9,0},... | collective-permute-start | bytes 110600 | tf_op jit(solution)/shard_map/ppermute | solution.py:198
  19.6 1.6 %collective-permute-done.3.refs_3_ = f32[72,128]{1,0:T(8,128)S(1)} collective-permute-done((f32[72,128]{1,0:T(8,128)S(1)}, f32[72,128]{1,0:T(8,128)S(1)}, u32[]{:S(2)}, u32[]{:S(2)}) %collective-permute-start.3) | collective-permute-done | bytes 36896 | tf_op jit(solution)/shard_map/ppermute | solution.py:198
  21.3 1.8 %collective-permute-start.4 = (f32[40,128]{1,0:T(8,128)S(1)}, f32[40,128]{1,0:T(8,128)S(1)}, u32[]{:S(2)}, u32[]{:S(2)}) collective-permute-start(f32[40,128]{1,0:T(8,128)S(1)} %fusion.7), channel_id=1, source_target_pairs={{0,17},{1,16},{2,19},{3,18},{4,21},{5,20},{6,23},{7,22},{8,25},{9,... | collective-permute-start | bytes 61448 | tf_op jit(solution)/shard_map/ppermute | solution.py:198
  23.2 1.6 %collective-permute-done.4.refs_4_ = f32[40,128]{1,0:T(8,128)S(1)} collective-permute-done((f32[40,128]{1,0:T(8,128)S(1)}, f32[40,128]{1,0:T(8,128)S(1)}, u32[]{:S(2)}, u32[]{:S(2)}) %collective-permute-start.4) | collective-permute-done | bytes 20512 | tf_op jit(solution)/shard_map/ppermute | solution.py:198
  24.8 1.8 %second.1 = (f32[64,1024]{1,0:T(8,128)S(1)}, f32[64,1024]{1,0:T(8,128)S(1)}, f32[64,1024]{1,0:T(8,128)S(1)}, f32[168,128]{1,0:T(8,128)S(1)}) custom-call(f32[8,128]{1,0:T(8,128)S(1)} %fusion.19.tail_ref.old_ref, f32[168,128]{1,0:T(8,128)S(1)} %collective-permute-done.refs_0_, f32[136,128]{1,0:T(8,128)S(1)} %collective-permute-done.1.refs_1_, ...), custom_call_target="tpu_custom_call" | custom-call | tf_op jit(solution)/shard_map/second/pallas_call | solution.py:240
  26.6 0.2 collective-permute-start.5
  26.8 1.2 %collective-permute-done.5.refs_0_ = f32[168,128]{1,0:T(8,128)S(1)} collective-permute-done((f32[168,128]{1,0:T(8,128)S(1)}, f32[168,128]{1,0:T(8,128)S(1)}, u32[]{:S(2)}, u32[]{:S(2)}) %collective-permute-start.5) | collective-permute-done | bytes 86048 | tf_op jit(solution)/shard_map/ppermute | solution.py:198
  28.0 1.3 %collective-permute-start.6 = (f32[136,128]{1,0:T(8,128)S(1)}, f32[136,128]{1,0:T(8,128)S(1)}, u32[]{:S(2)}, u32[]{:S(2)}) collective-permute-start(f32[136,128]{1,0:T(8,128)S(1)} %fusion), channel_id=1, source_target_pairs={{0,3},{1,2},{2,1},{3,0},{4,7},{5,6},{6,5},{7,4},{8,11},{9,10},{10,... | collective-permute-start | bytes 208904 | tf_op jit(solution)/shard_map/ppermute | solution.py:198
  29.3 2.9 %collective-permute-done.6.refs_1_ = f32[136,128]{1,0:T(8,128)S(1)} collective-permute-done((f32[136,128]{1,0:T(8,128)S(1)}, f32[136,128]{1,0:T(8,128)S(1)}, u32[]{:S(2)}, u32[]{:S(2)}) %collective-permute-start.6) | collective-permute-done | bytes 69664 | tf_op jit(solution)/shard_map/ppermute | solution.py:198
  32.3 2.6 %collective-permute-start.7 = (f32[104,128]{1,0:T(8,128)S(1)}, f32[104,128]{1,0:T(8,128)S(1)}, u32[]{:S(2)}, u32[]{:S(2)}) collective-permute-start(f32[104,128]{1,0:T(8,128)S(1)} %fusion.2), channel_id=1, source_target_pairs={{0,5},{1,4},{2,7},{3,6},{4,1},{5,0},{6,3},{7,2},{8,13},{9,12},{10,... | collective-permute-start | bytes 159752 | tf_op jit(solution)/shard_map/ppermute | solution.py:198
  34.9 2.2 %collective-permute-done.7.refs_2_ = f32[104,128]{1,0:T(8,128)S(1)} collective-permute-done((f32[104,128]{1,0:T(8,128)S(1)}, f32[104,128]{1,0:T(8,128)S(1)}, u32[]{:S(2)}, u32[]{:S(2)}) %collective-permute-start.7) | collective-permute-done | bytes 53280 | tf_op jit(solution)/shard_map/ppermute | solution.py:198
  37.1 1.2 %collective-permute-start.8 = (f32[72,128]{1,0:T(8,128)S(1)}, f32[72,128]{1,0:T(8,128)S(1)}, u32[]{:S(2)}, u32[]{:S(2)}) collective-permute-start(f32[72,128]{1,0:T(8,128)S(1)} %fusion.4), channel_id=1, source_target_pairs={{0,9},{1,8},{2,11},{3,10},{4,13},{5,12},{6,15},{7,14},{8,1},{9,0},... | collective-permute-start | bytes 110600 | tf_op jit(solution)/shard_map/ppermute | solution.py:198
  38.3 2.3 %collective-permute-done.8.refs_3_ = f32[72,128]{1,0:T(8,128)S(1)} collective-permute-done((f32[72,128]{1,0:T(8,128)S(1)}, f32[72,128]{1,0:T(8,128)S(1)}, u32[]{:S(2)}, u32[]{:S(2)}) %collective-permute-start.8) | collective-permute-done | bytes 36896 | tf_op jit(solution)/shard_map/ppermute | solution.py:198
  40.6 1.2 %collective-permute-start.9 = (f32[40,128]{1,0:T(8,128)S(1)}, f32[40,128]{1,0:T(8,128)S(1)}, u32[]{:S(2)}, u32[]{:S(2)}) collective-permute-start(f32[40,128]{1,0:T(8,128)S(1)} %fusion.6), channel_id=1, source_target_pairs={{0,17},{1,16},{2,19},{3,18},{4,21},{5,20},{6,23},{7,22},{8,25},{9,... | collective-permute-start | bytes 61448 | tf_op jit(solution)/shard_map/ppermute | solution.py:198
  41.8 2.1 %collective-permute-done.9.refs_4_ = f32[40,128]{1,0:T(8,128)S(1)} collective-permute-done((f32[40,128]{1,0:T(8,128)S(1)}, f32[40,128]{1,0:T(8,128)S(1)}, u32[]{:S(2)}, u32[]{:S(2)}) %collective-permute-start.9) | collective-permute-done | bytes 20512 | tf_op jit(solution)/shard_map/ppermute | solution.py:198
  43.9 2.1 %third.1 = (f32[64,1024]{1,0:T(8,128)}, f32[64,1024]{1,0:T(8,128)}) custom-call(s32[1,1024]{1,0:T(1,128)S(1)} %get-tuple-element.14.order_ref, f32[8,128]{1,0:T(8,128)S(1)} %fusion.19.tail_ref.old_ref, f32[8,128]{1,0:T(8,128)S(1)} %fusion.18.tail_ref, f32[168,128]{1,0:T(8,128)S(1)} %collective-permute-done.5.refs_0_, ...), custom_call_target="tpu_custom_call" | custom-call | tf_op jit(solution)/shard_map/third/pallas_call | solution.py:249
  (30 shorter events, 0.4 us)
Async XLA Ops:
  5.3 1.5 %collective-permute-start = (f32[168,128]{1,0:T(8,128)S(1)}, f32[168,128]{1,0:T(8,128)S(1)}, u32[]{:S(2)}, u32[]{:S(2)}) collective-permute-start(f32[168,128]{1,0:T(8,128)S(1)} %get-tuple-element.15), channel_id=1, source_target_pairs={{0,1},{1,0},{2,3},{3,2},{4,5},{5,4},{6,7},{7,6},{8,9},{9,8},{10,11... | collective-permute-start | bytes 258056 | tf_op jit(solution)/shard_map/ppermute | solution.py:198
  6.8 5.0 %collective-permute-start.1 = (f32[136,128]{1,0:T(8,128)S(1)}, f32[136,128]{1,0:T(8,128)S(1)}, u32[]{:S(2)}, u32[]{:S(2)}) collective-permute-start(f32[136,128]{1,0:T(8,128)S(1)} %fusion.1), channel_id=1, source_target_pairs={{0,3},{1,2},{2,1},{3,0},{4,7},{5,6},{6,5},{7,4},{8,11},{9,10},{10,... | collective-permute-start | bytes 208904 | tf_op jit(solution)/shard_map/ppermute | solution.py:198
  11.8 4.9 %collective-permute-start.2 = (f32[104,128]{1,0:T(8,128)S(1)}, f32[104,128]{1,0:T(8,128)S(1)}, u32[]{:S(2)}, u32[]{:S(2)}) collective-permute-start(f32[104,128]{1,0:T(8,128)S(1)} %fusion.3), channel_id=1, source_target_pairs={{0,5},{1,4},{2,7},{3,6},{4,1},{5,0},{6,3},{7,2},{8,13},{9,12},{10,... | collective-permute-start | bytes 159752 | tf_op jit(solution)/shard_map/ppermute | solution.py:198
  16.7 4.6 %collective-permute-start.3 = (f32[72,128]{1,0:T(8,128)S(1)}, f32[72,128]{1,0:T(8,128)S(1)}, u32[]{:S(2)}, u32[]{:S(2)}) collective-permute-start(f32[72,128]{1,0:T(8,128)S(1)} %fusion.5), channel_id=1, source_target_pairs={{0,9},{1,8},{2,11},{3,10},{4,13},{5,12},{6,15},{7,14},{8,1},{9,0},... | collective-permute-start | bytes 110600 | tf_op jit(solution)/shard_map/ppermute | solution.py:198
  21.3 3.5 %collective-permute-start.4 = (f32[40,128]{1,0:T(8,128)S(1)}, f32[40,128]{1,0:T(8,128)S(1)}, u32[]{:S(2)}, u32[]{:S(2)}) collective-permute-start(f32[40,128]{1,0:T(8,128)S(1)} %fusion.7), channel_id=1, source_target_pairs={{0,17},{1,16},{2,19},{3,18},{4,21},{5,20},{6,23},{7,22},{8,25},{9,... | collective-permute-start | bytes 61448 | tf_op jit(solution)/shard_map/ppermute | solution.py:198
  26.6 1.3 %collective-permute-start.5 = (f32[168,128]{1,0:T(8,128)S(1)}, f32[168,128]{1,0:T(8,128)S(1)}, u32[]{:S(2)}, u32[]{:S(2)}) collective-permute-start(f32[168,128]{1,0:T(8,128)S(1)} %get-tuple-element.22), channel_id=1, source_target_pairs={{0,1},{1,0},{2,3},{3,2},{4,5},{5,4},{6,7},{7,6},{8,9},{9,8},{10,11... | collective-permute-start | bytes 258056 | tf_op jit(solution)/shard_map/ppermute | solution.py:198
  28.0 4.2 %collective-permute-start.6 = (f32[136,128]{1,0:T(8,128)S(1)}, f32[136,128]{1,0:T(8,128)S(1)}, u32[]{:S(2)}, u32[]{:S(2)}) collective-permute-start(f32[136,128]{1,0:T(8,128)S(1)} %fusion), channel_id=1, source_target_pairs={{0,3},{1,2},{2,1},{3,0},{4,7},{5,6},{6,5},{7,4},{8,11},{9,10},{10,... | collective-permute-start | bytes 208904 | tf_op jit(solution)/shard_map/ppermute | solution.py:198
  32.3 4.8 %collective-permute-start.7 = (f32[104,128]{1,0:T(8,128)S(1)}, f32[104,128]{1,0:T(8,128)S(1)}, u32[]{:S(2)}, u32[]{:S(2)}) collective-permute-start(f32[104,128]{1,0:T(8,128)S(1)} %fusion.2), channel_id=1, source_target_pairs={{0,5},{1,4},{2,7},{3,6},{4,1},{5,0},{6,3},{7,2},{8,13},{9,12},{10,... | collective-permute-start | bytes 159752 | tf_op jit(solution)/shard_map/ppermute | solution.py:198
  37.1 3.5 %collective-permute-start.8 = (f32[72,128]{1,0:T(8,128)S(1)}, f32[72,128]{1,0:T(8,128)S(1)}, u32[]{:S(2)}, u32[]{:S(2)}) collective-permute-start(f32[72,128]{1,0:T(8,128)S(1)} %fusion.4), channel_id=1, source_target_pairs={{0,9},{1,8},{2,11},{3,10},{4,13},{5,12},{6,15},{7,14},{8,1},{9,0},... | collective-permute-start | bytes 110600 | tf_op jit(solution)/shard_map/ppermute | solution.py:198
  40.6 3.3 %collective-permute-start.9 = (f32[40,128]{1,0:T(8,128)S(1)}, f32[40,128]{1,0:T(8,128)S(1)}, u32[]{:S(2)}, u32[]{:S(2)}) collective-permute-start(f32[40,128]{1,0:T(8,128)S(1)} %fusion.6), channel_id=1, source_target_pairs={{0,17},{1,16},{2,19},{3,18},{4,21},{5,20},{6,23},{7,22},{8,25},{9,... | collective-permute-start | bytes 61448 | tf_op jit(solution)/shard_map/ppermute | solution.py:198

commit v3 on v0

v3 whole, which is shorter than its diff:
```python
import jax
import jax.numpy as jnp
from jax import lax
from jax.experimental import pallas as pl
from jax.experimental.pallas import tpu as pltpu
from jax.sharding import PartitionSpec as P

AXES = ("wide", "narrow")
F32 = jnp.float32
BF16 = jnp.bfloat16
TAIL = 8
FLOPS = 2 * 10**9
VMEM = pl.BlockSpec(memory_space=pltpu.VMEM)
HBM = pl.BlockSpec(memory_space=pltpu.HBM)


def dot(a, b):
    return jnp.dot(a, b, preferred_element_type=F32)


def dot_nt(a, b):
    return lax.dot_general(a, b, (((1,), (1,)), ((), ())), preferred_element_type=F32)


def split2(value):
    high = value.astype(BF16)
    return high, (value - high.astype(F32)).astype(BF16)


def iota(shape, axis):
    return lax.broadcasted_iota(jnp.int32, shape, axis)


def to_row(column, lanes):
    shape = (column.shape[0], lanes)
    return jnp.sum(jnp.where(iota(shape, 0) == iota(shape, 1), column, 0.0), axis=0, keepdims=True)


def to_column(row, rows):
    shape = (rows, row.shape[1])
    return jnp.sum(jnp.where(iota(shape, 0) == lax.rem(iota(shape, 1), rows), row, 0.0), axis=1, keepdims=True)


def own_side():
    index = lax.axis_index("wide") * lax.axis_size("narrow") + lax.axis_index("narrow")
    side = index & 1
    for bit in range(1, (lax.axis_size("wide") * lax.axis_size("narrow")).bit_length() - 1):
        side = side ^ ((index >> bit) & 1)
    return side


def write_projection(msg_ref, own_ref, q_hi, q_lo, both, levels, rhs):
    quarter = rhs // 2
    full = dot_nt(q_hi, both) + dot_nt(q_lo, both)
    full = full + pltpu.roll(full, rhs, 1)
    rows = own_ref.shape[0]
    blocks = [full[group * rows:(group + 1) * rows] for group in range(4)]
    group = iota((rows, 2 * rhs), 1) // quarter
    lower = jnp.where((group & 1) == 0, jnp.where(group < 2, blocks[0], blocks[2]),
                      jnp.where(group < 2, pltpu.roll(blocks[1], quarter, 1), pltpu.roll(blocks[3], quarter, 1)))
    back = 2 * rhs - quarter
    upper = jnp.where((group & 1) == 1, jnp.where(group < 2, blocks[1], blocks[3]),
                      jnp.where(group < 2, pltpu.roll(blocks[0], back, 1), pltpu.roll(blocks[2], back, 1)))
    first = full[4 * rows:]
    half = first.shape[0] // 2
    msg_ref[:half] = jnp.where(iota((half, 2 * rhs), 1) < rhs, first[:half], first[half:])
    even = own_side() == 0
    own_ref[...] = jnp.where(even, lower, upper)
    msg_ref[half:] = jnp.where(even, upper, lower)


def near_product(both, field_hi, d_hi, d_lo, rhs):
    wide = dot(both, d_hi)
    return wide[:rhs] + wide[rhs:] + dot(field_hi, d_lo)


def write_tail(tail_ref, field, near):
    shape = tail_ref.shape
    square = to_row(jnp.sum(field * field, axis=1, keepdims=True), shape[1])
    product = to_row(jnp.sum(field * near, axis=1, keepdims=True), shape[1])
    index = iota(shape, 0)
    tail_ref[...] = jnp.where(index == 0, square, jnp.where(index == 1, product, 0.0))


def far_product(zero_ref, own_ref, other_ref, q_hi, q_lo, rhs):
    lanes = 2 * rhs
    quarter = rhs // 2
    rows = own_ref.shape[0] - TAIL
    even = own_side() == 0
    own, other = own_ref[:rows], other_ref[:rows]
    lower, upper = jnp.where(even, own, other), jnp.where(even, other, own)
    lane = iota((rows, lanes), 1)
    pieces = []
    for group in range(4):
        left = pltpu.roll(lower, (lanes - group * quarter) % lanes, 1) if group else lower
        right = pltpu.roll(upper, (lanes + quarter - group * quarter) % lanes, 1) if group != 1 else upper
        pieces.append(jnp.where(lane < quarter, left, right))
    zero = zero_ref[:own_half(q_hi, rows)]
    pieces += [zero, pltpu.roll(zero, rhs, 1)]
    turned = jnp.concatenate(pieces, axis=0).T[:rhs]
    hi, lo = split2(turned)
    wide = dot(jnp.concatenate([hi, lo], axis=0), q_hi)
    return wide[:rhs] + wide[rhs:] + dot(hi, q_lo)


def own_half(q_hi, rows):
    return (q_hi.shape[0] - 4 * rows) // 2


def scalars(own_ref, other_ref, rhs):
    rows = own_ref.shape[0] - TAIL
    own, other = own_ref[rows:], other_ref[rows:]
    both = own + other
    norm = to_column(both[0:1], rhs)
    product = to_column(both[1:2], rhs)
    quarter = rhs // 2
    shape = (rhs, own.shape[1])
    row = iota(shape, 0)
    mine = (row // quarter) == own_side()
    cross = jnp.where(mine, own[2:3], other[2:3])
    cross = jnp.where(lax.rem(iota(shape, 1), quarter) == lax.rem(row, quarter), cross, 0.0)
    return norm, product + jnp.sum(cross, axis=1, keepdims=True)


def start_kernel(order_hbm, rs_hbm, f_hbm, b_ref, msg_ref, own_ref, qhi_ref, qlo_ref, order_ref, rs_ref, f_ref, sems):
    levels, rank, leaf = f_ref.shape
    rhs = rs_ref.shape[0]
    chunk = 256
    copies = [
        pltpu.make_async_copy(order_hbm, order_ref, sems.at[0]),
        pltpu.make_async_copy(rs_hbm, rs_ref, sems.at[1]),
        pltpu.make_async_copy(f_hbm, f_ref, sems.at[2]),
    ]
    for copy in copies:
        copy.start()
    for copy in copies:
        copy.wait()
    two = jnp.concatenate(split2(rs_ref[...]), axis=0)
    local_order = lax.rem(order_ref[...], leaf)
    for n in range(leaf // chunk):
        cols = pl.ds(n * chunk, chunk)
        onehot = jnp.where(iota((leaf, chunk), 0) == local_order[:, n * chunk:(n + 1) * chunk], 1.0, 0.0).astype(BF16)
        got = dot(two, onehot)
        b_ref[:, cols] = got[:rhs] + got[rhs:]
    block = rank // 4
    for level in range(levels):
        for group in range(4):
            hi, lo = split2(f_ref[level, pl.ds(group * block, block)])
            if level:
                rows = pl.ds((group * (levels - 1) + level - 1) * block, block)
            else:
                rows = pl.ds((4 * (levels - 1) + group) * block, block)
            qhi_ref[rows] = hi
            qlo_ref[rows] = lo
    both = jnp.concatenate(split2(b_ref[...]), axis=0)
    write_projection(msg_ref, own_ref, qhi_ref[...], qlo_ref[...], both, levels, rhs)


def near_kernel(b_ref, d_ref, near_ref, tail_ref, dhi_ref, dlo_ref):
    rhs, leaf = b_ref.shape
    chunk = 256
    field = b_ref[...]
    field_hi, field_lo = split2(field)
    both = jnp.concatenate([field_hi, field_lo], axis=0)
    for n in range(leaf // chunk):
        cols = pl.ds(n * chunk, chunk)
        d_hi, d_lo = split2(d_ref[:, cols])
        dhi_ref[:, cols] = d_hi
        dlo_ref[:, cols] = d_lo
        near_ref[:, cols] = near_product(both, field_hi, dhi_ref[:, cols], dlo_ref[:, cols], rhs)
    write_tail(tail_ref, field, near_ref[...])


def step_kernel(zero_ref, own_ref, other_ref, b_ref, near_ref, qhi_ref, qlo_ref, r_ref, image_ref, msg_ref, mine_ref):
    rhs = b_ref.shape[0]
    levels = mine_ref.shape[0] // (qhi_ref.shape[0] // 4 - mine_ref.shape[0]) + 1
    norm, product = scalars(own_ref, other_ref, rhs)
    alpha = norm / product
    far = far_product(zero_ref, own_ref, other_ref, qhi_ref[...], qlo_ref[...], rhs)
    image = near_ref[...] + far
    image_ref[...] = image
    field = b_ref[...] - alpha * image
    r_ref[...] = field
    both = jnp.concatenate(split2(field), axis=0)
    write_projection(msg_ref, mine_ref, qhi_ref[...], qlo_ref[...], both, levels, rhs)


def again_kernel(r_ref, dhi_ref, dlo_ref, near_ref, tail_ref):
    rhs = r_ref.shape[0]
    field = r_ref[...]
    field_hi, field_lo = split2(field)
    both = jnp.concatenate([field_hi, field_lo], axis=0)
    near = near_product(both, field_hi, dhi_ref[...], dlo_ref[...], rhs)
    near_ref[...] = near
    write_tail(tail_ref, field, near)


def last_kernel(order_ref, zero_ref, own_ref, other_ref, old_own_ref, old_other_ref, b_ref, image_ref, r_ref, near_ref,
                qhi_ref, qlo_ref, x_out, r_out):
    rhs, leaf = b_ref.shape
    norm_old, product_old = scalars(old_own_ref, old_other_ref, rhs)
    alpha_old = norm_old / product_old
    norm, product = scalars(own_ref, other_ref, rhs)
    ratio = norm / norm_old
    alpha = norm / (product - ratio * norm / alpha_old)
    far = far_product(zero_ref, own_ref, other_ref, qhi_ref[...], qlo_ref[...], rhs)
    direction = r_ref[...] + ratio * b_ref[...]
    along = near_ref[...] + far + ratio * image_ref[...]
    x = alpha_old * b_ref[...] + alpha * direction
    r = r_ref[...] - alpha * along
    four = jnp.concatenate(split2(x) + split2(r), axis=0)
    chunk = 256
    local_order = lax.rem(order_ref[...], leaf)
    for n in range(leaf // chunk):
        cols = pl.ds(n * chunk, chunk)
        index = iota((chunk, leaf), 0) + n * chunk
        onehot = jnp.where(index == local_order, 1.0, 0.0).astype(BF16)
        got = dot_nt(four, onehot)
        x_out[:, cols] = got[:rhs] + got[rhs:2 * rhs]
        r_out[:, cols] = got[2 * rhs:3 * rhs] + got[3 * rhs:]


def swapped(value, mask):
    mask = mask ^ (mask.bit_count() & 1 if mask > 1 else 0)
    count = lax.axis_size("wide") * lax.axis_size("narrow")
    return lax.ppermute(value, AXES, [(source, source ^ mask) for source in range(count)])


def column_products(left, right):
    return jnp.sum(left * right, axis=0, keepdims=True)


def with_row(merged, row, place):
    return merged + jnp.pad(row, ((merged.shape[0] - TAIL + place, TAIL - place - 1), (0, 0)))


def butterfly(first, own, tail_of, levels, rank):
    half, part = rank // 2, rank // 4
    got = swapped(first, 1)
    tail = with_row(tail_of(), column_products(first[:half], got[:half]), 1)
    message = jnp.concatenate([own + got[half:], tail])
    parts = []
    level = 1
    low = lax.axis_size("narrow").bit_length() - 1
    while level < levels:
        if level < low or level + 1 == levels:
            other = swapped(message, 2**level)
            parts.append(other[:part])
            cross = 2.0 * column_products(message[:part], other[:part])
            message = with_row(message[part:] + other[part:], cross, 2)
            level += 1
        else:
            x = swapped(message, 2**level)
            y = swapped(message, 2 * 2**level)
            z = swapped(message, 3 * 2**level)
            far = y + z
            pair = message[part:] + x[part:]
            parts += [x[:part], far[part:2 * part]]
            cross = column_products(message[:part], x[:part]) + column_products(y[:part], z[:part])
            cross = 2.0 * (cross + column_products(pair[:part], far[part:2 * part]))
            message = with_row(pair[part:] + far[2 * part:], cross, 2)
            level += 2
    mine = jnp.concatenate(parts + [message])
    return got, mine, swapped(mine, 1)


def call(kernel, name, outs, in_specs, scratch=(), flops=0):
    return pl.pallas_call(
        kernel,
        out_shape=outs,
        in_specs=in_specs,
        out_specs=tuple(VMEM for _ in outs),
        scratch_shapes=list(scratch),
        compiler_params=pltpu.CompilerParams(vmem_limit_bytes=32 * 1024 * 1024),
        cost_estimate=pl.CostEstimate(flops=flops, bytes_accessed=0, transcendentals=0) if flops else None,
        name=name,
    )


def local(right_side, leaf_blocks, factors, leaf_order):
    leaf = leaf_blocks.shape[1]
    levels, rank, _ = factors.shape
    rhs = right_side.shape[0]
    lanes = 2 * rhs
    rows = (levels - 1) * rank // 4
    pinned = [pltpu.with_memory_space_constraint(value, pltpu.HBM) for value in (leaf_order.reshape(1, leaf), right_side, factors)]
    field = jax.ShapeDtypeStruct((rhs, leaf), F32)
    message = jax.ShapeDtypeStruct((rank // 2 + rows, lanes), F32)
    own = jax.ShapeDtypeStruct((rows, lanes), F32)
    tail = jax.ShapeDtypeStruct((TAIL, lanes), F32)
    matrix = jax.ShapeDtypeStruct((leaf, leaf), BF16)
    basis = jax.ShapeDtypeStruct((levels * rank, leaf), BF16)
    scratch = [pltpu.VMEM(right_side.shape, F32), pltpu.VMEM(factors.shape, F32), pltpu.SemaphoreType.DMA((3,))]
    b, first, mine, qhi, qlo, order = call(
        start_kernel, "start", (field, message, own, basis, basis, jax.ShapeDtypeStruct((1, leaf), jnp.int32)),
        [HBM] * 3, scratch)(*pinned)
    kept = {}

    def first_tail():
        kept["near"], value, kept["dhi"], kept["dlo"] = call(
            near_kernel, "near", (field, tail, matrix, matrix), [VMEM] * 2, flops=FLOPS)(b, leaf_blocks)
        return value

    zero, ours, theirs = butterfly(first, mine, first_tail, levels, rank)
    r, image, first, mine = call(step_kernel, "step", (field, field, message, own), [VMEM] * 7)(
        zero, ours, theirs, b, kept["near"], qhi, qlo)

    def next_tail():
        kept["next"], value = call(again_kernel, "again", (field, tail), [VMEM] * 3, flops=FLOPS)(r, kept["dhi"], kept["dlo"])
        return value

    zero, ours_next, theirs_next = butterfly(first, mine, next_tail, levels, rank)
    return call(last_kernel, "last", (field, field), [VMEM] * 12)(
        order, zero, ours_next, theirs_next, ours, theirs, b, image, r, kept["next"], qhi, qlo)


def solution(mesh):
    placed = (
        P(None, AXES),
        P(AXES, None),
        P(None, None, AXES),
        P(AXES),
    )
    return jax.shard_map(
        local,
        mesh=mesh,
        in_specs=placed,
        out_specs=(P(None, AXES), P(None, AXES)),
        check_vma=False,
    )
```

time: 75.6 us -> 43.5 us (0.58)
  matrix products: 13 us -> 0 us
  local copies, waits for them, and re-layouts: 13.1 us -> 2.19 us
  waiting for transfers between devices: 24.8 us -> 16.3 us
  Pallas kernels: 0 us -> 7.42 us
  starting transfers between devices: 22.1 us -> 16.2 us
  other arithmetic: 1.48 us -> 0.41 us
    dot_general x6 -> x0, matrix products: 13 us -> none  [the longest x2 7.69 us: kernel_with_sums(): jnp.dot(vector, leaf_blocks, precision=HIGH, preferred_element_type=jnp.f...]
    ppermute x20 -> x14, waiting for transfers between devices: 24.8 us -> 16.3 us  [swapped(): lax.ppermute(value, AXES, [(source, source ^ mask) for source in range(co...]
    pallas_call x0 -> x5, Pallas kernels: none -> 7.42 us  [the longest x1 2.43 us: local(): call(start_kernel, 'start', (field, message, own, basis, basis, jax.Shape...]
    scatter x2 -> x0, local copies, waits for them, and re-layouts: 6.61 us -> none  [the longest x1 3.39 us: local(): placed_sol = jnp.zeros_like(right_side).at[:, local_order].set(solution)]
    ppermute x20 -> x14, starting transfers between devices: 22.1 us -> 16.2 us  [swapped(): lax.ppermute(value, AXES, [(source, source ^ mask) for source in range(co...]
    gather x2 -> x0, local copies, waits for them, and re-layouts: 2.99 us -> none  [local(): rhs_leaf = jnp.take(right_side, local_order, axis=1)]
    unnamed x9 -> x2, local copies, waits for them, and re-layouts: 3.1 us -> 2.19 us
    and x1 -> x0, other arithmetic: 0.8 us -> none  [local(): rhs_leaf = jnp.take(right_side, local_order, axis=1)]
  transfers between devices with their start and end apart: 20 -> 14, of which waited for: 11 -> 12; matrix products, arithmetic and copies ran while one was open for 7% -> 0% of each run, Pallas kernels for 0% -> 4%
where the time goes in v3:
time: 43.5 us; the launch traced here: 43.3 us
  waiting for transfers between devices  16.3 us (37%)
  starting transfers between devices  16.2 us (37%)
  Pallas kernels  7.42 us (17%)
  local copies, waits for them, and re-layouts  2.19 us (5%)
  between operations  0.73 us (2%)
    ppermute x14, waiting for transfers between devices, swapped(): lax.ppermute(value, AXES, [(source, source ^ mask) for source in range(co...  16.3 us
    ppermute x14, starting transfers between devices, swapped(): lax.ppermute(value, AXES, [(source, source ^ mask) for source in range(co...  16.2 us
    pallas_call x1, Pallas kernels, local(): call(start_kernel, 'start', (field, message, own, basis, basis, jax.Shape...  2.43 us
    unnamed x2, local copies, waits for them, and re-layouts  2.19 us
    pallas_call x1, Pallas kernels, local(): call(last_kernel, 'last', (field, field), [VMEM] * 12)  1.95 us
    pallas_call x1, Pallas kernels, local(): call(step_kernel, 'step', (field, field, message, own), [VMEM] * 7)  1.11 us
    pallas_call x1, Pallas kernels, first_tail(): call(near_kernel, 'near', (field, tail, matrix, matrix), [VMEM] * 2, flop...  1.08 us
  transfers between devices with their start and end apart: 14, of which 12 were waited for; matrix products, arithmetic and copies ran while one was open for 0% of the time, Pallas kernels for 4%

profile of v3, /device:TPU:0, one launch (start us, length us, event | category | flops | bytes accessed | tf_op | source)
XLA Modules:
  0.0 43.3 jit_solution(13078654768570365660)
XLA Ops:
  0.6 2.4 %start.1 = (f32[64,1024]{1,0:T(8,128)S(1)}, f32[96,128]{1,0:T(8,128)S(1)}, f32[64,128]{1,0:T(8,128)S(1)}, bf16[320,1024]{1,0:T(8,128)(2,1)S(1)}, bf16[320,1024]{1,0:T(8,128)(2,1)S(1)}, /*index=5*/s32[1,1024]{1,0:T(1,128)S(1)}) custom-call(s32[1,1024]{1,0:T(1,128)} %bitcast.15, f32[64,1024]{1,0:T(8,128)} %rs_hbm.1, f32[5,64,1024]{2,1,0:T(8,128)} %f_hbm.1), custom_call_target="tpu_custom_call" | custom-call | tf_op jit(solution)/shard_map/start/pallas_call | solution.py:294
  3.1 0.6 %collective-permute-start = (f32[96,128]{1,0:T(8,128)S(1)}, f32[96,128]{1,0:T(8,128)S(1)}, u32[]{:S(2)}, u32[]{:S(2)}) collective-permute-start(f32[96,128]{1,0:T(8,128)S(1)} %get-tuple-element.19), channel_id=1, source_target_pairs={{0,1},{1,0},{2,3},{3,2},{4,5},{5,4},{6,7},{7,6},{8,9},{9,8},{10,11... | collective-permute-start | bytes 147464 | tf_op jit(solution)/shard_map/ppermute | solution.py:226
  3.6 0.0 copy-start
  3.6 2.2 %copy-done = f32[1024,1024]{1,0:T(8,128)S(1)} copy-done((f32[1024,1024]{1,0:T(8,128)S(1)}, f32[1024,1024]{1,0:T(8,128)}, u32[]{:S(2)}) %copy-start) | copy-done | bytes 4194328
  5.8 1.1 %near.1 = (f32[64,1024]{1,0:T(8,128)S(1)}, f32[8,128]{1,0:T(8,128)S(1)}, bf16[1024,1024]{1,0:T(8,128)(2,1)S(1)}, bf16[1024,1024]{1,0:T(8,128)(2,1)S(1)}) custom-call(f32[64,1024]{1,0:T(8,128)S(1)} %get-tuple-element.21.b_ref, f32[1024,1024]{1,0:T(8,128)S(1)} %copy-done), custom_call_target="tpu_custom_call" | custom-call | flops 2000000000 | tf_op jit(solution)/shard_map/near/pallas_call | solution.py:300
  6.9 0.0 collective-permute-done.zero_ref
  7.0 2.8 %collective-permute-start.1 = (f32[72,128]{1,0:T(8,128)S(1)}, f32[72,128]{1,0:T(8,128)S(1)}, u32[]{:S(2)}, u32[]{:S(2)}) collective-permute-start(f32[72,128]{1,0:T(8,128)S(1)} %pad_maximum_fusion), channel_id=1, source_target_pairs={{0,3},{1,2},{2,1},{3,0},{4,7},{5,6},{6,5},{7,4},{8,11},{9,10},{10,... | collective-permute-start | bytes 110600 | tf_op jit(solution)/shard_map/ppermute | solution.py:226
  9.7 1.8 %collective-permute-done.1 = f32[72,128]{1,0:T(8,128)S(1)} collective-permute-done((f32[72,128]{1,0:T(8,128)S(1)}, f32[72,128]{1,0:T(8,128)S(1)}, u32[]{:S(2)}, u32[]{:S(2)}) %collective-permute-start.1) | collective-permute-done | bytes 36896 | tf_op jit(solution)/shard_map/ppermute | solution.py:226
  11.6 2.6 %collective-permute-start.2 = (f32[56,128]{1,0:T(8,128)S(1)}, f32[56,128]{1,0:T(8,128)S(1)}, u32[]{:S(2)}, u32[]{:S(2)}) collective-permute-start(f32[56,128]{1,0:T(8,128)S(1)} %fusion.5), channel_id=1, source_target_pairs={{0,5},{1,4},{2,7},{3,6},{4,1},{5,0},{6,3},{7,2},{8,13},{9,12},{10,... | collective-permute-start | bytes 86024 | tf_op jit(solution)/shard_map/ppermute | solution.py:226
  14.2 1.7 %collective-permute-done.2 = f32[56,128]{1,0:T(8,128)S(1)} collective-permute-done((f32[56,128]{1,0:T(8,128)S(1)}, f32[56,128]{1,0:T(8,128)S(1)}, u32[]{:S(2)}, u32[]{:S(2)}) %collective-permute-start.2) | collective-permute-done | bytes 28704 | tf_op jit(solution)/shard_map/ppermute | solution.py:226
  15.9 1.5 %collective-permute-start.3 = (f32[40,128]{1,0:T(8,128)S(1)}, f32[40,128]{1,0:T(8,128)S(1)}, u32[]{:S(2)}, u32[]{:S(2)}) collective-permute-start(f32[40,128]{1,0:T(8,128)S(1)} %fusion.7), channel_id=1, source_target_pairs={{0,9},{1,8},{2,11},{3,10},{4,13},{5,12},{6,15},{7,14},{8,1},{9,0},... | collective-permute-start | bytes 61448 | tf_op jit(solution)/shard_map/ppermute | solution.py:226
  17.4 1.5 %collective-permute-start.5 = (f32[40,128]{1,0:T(8,128)S(1)}, f32[40,128]{1,0:T(8,128)S(1)}, u32[]{:S(2)}, u32[]{:S(2)}) collective-permute-start(f32[40,128]{1,0:T(8,128)S(1)} %fusion.7), channel_id=1, source_target_pairs={{0,24},{1,25},{2,26},{3,27},{4,28},{5,29},{6,30},{7,31},{8,16},{9,... | collective-permute-start | bytes 61448 | tf_op jit(solution)/shard_map/ppermute | solution.py:226
  18.9 0.0 collective-permute-start.4
  18.9 0.3 collective-permute-done.3
  19.2 3.0 %collective-permute-done.5 = f32[40,128]{1,0:T(8,128)S(1)} collective-permute-done((f32[40,128]{1,0:T(8,128)S(1)}, f32[40,128]{1,0:T(8,128)S(1)}, u32[]{:S(2)}, u32[]{:S(2)}) %collective-permute-start.5) | collective-permute-done | bytes 20512 | tf_op jit(solution)/shard_map/ppermute | solution.py:226
  22.2 0.3 collective-permute-done.4
  22.6 0.2 collective-permute-start.6
  22.8 1.1 %collective-permute-done.6.other_ref.old_other_ref = f32[72,128]{1,0:T(8,128)S(1)} collective-permute-done((f32[72,128]{1,0:T(8,128)S(1)}, f32[72,128]{1,0:T(8,128)S(1)}, u32[]{:S(2)}, u32[]{:S(2)}) %collective-permute-start.6) | collective-permute-done | bytes 36896 | tf_op jit(solution)/shard_map/ppermute | solution.py:226
  23.9 1.1 %step.1 = (f32[64,1024]{1,0:T(8,128)S(1)}, f32[64,1024]{1,0:T(8,128)S(1)}, f32[96,128]{1,0:T(8,128)S(1)}, f32[64,128]{1,0:T(8,128)S(1)}) custom-call(f32[96,128]{1,0:T(8,128)S(1)} %collective-permute-done.zero_ref, f32[72,128]{1,0:T(8,128)S(1)} %constant_dynamic-update-slice_fusion.own_ref.old_own_ref, ...), custom_call_target="tpu_custom_call" | custom-call | tf_op jit(solution)/shard_map/step/pallas_call | solution.py:305
  25.0 0.2 collective-permute-start.7
  25.2 0.9 %again.1 = (f32[64,1024]{1,0:T(8,128)S(1)}, f32[8,128]{1,0:T(8,128)S(1)}) custom-call(f32[64,1024]{1,0:T(8,128)S(1)} %get-tuple-element.28.r_ref, bf16[1024,1024]{1,0:T(8,128)(2,1)S(1)} %get-tuple-element.29.dhi_ref, bf16[1024,1024]{1,0:T(8,128)(2,1)S(1)} %get-tuple-element.30.dlo_ref), custom_call_target="tpu_custom_call" | custom-call | flops 2000000000 | tf_op jit(solution)/shard_map/again/pallas_call | solution.py:309
  26.1 0.2 collective-permute-done.7.zero_ref
  26.3 1.4 %collective-permute-start.8 = (f32[72,128]{1,0:T(8,128)S(1)}, f32[72,128]{1,0:T(8,128)S(1)}, u32[]{:S(2)}, u32[]{:S(2)}) collective-permute-start(f32[72,128]{1,0:T(8,128)S(1)} %pad_maximum_fusion.1), channel_id=1, source_target_pairs={{0,3},{1,2},{2,1},{3,0},{4,7},{5,6},{6,5},{7,4},{8,11},{9,10},{10,... | collective-permute-start | bytes 110600 | tf_op jit(solution)/shard_map/ppermute | solution.py:226
  27.8 2.1 %collective-permute-done.8 = f32[72,128]{1,0:T(8,128)S(1)} collective-permute-done((f32[72,128]{1,0:T(8,128)S(1)}, f32[72,128]{1,0:T(8,128)S(1)}, u32[]{:S(2)}, u32[]{:S(2)}) %collective-permute-start.8) | collective-permute-done | bytes 36896 | tf_op jit(solution)/shard_map/ppermute | solution.py:226
  29.9 2.4 %collective-permute-start.9 = (f32[56,128]{1,0:T(8,128)S(1)}, f32[56,128]{1,0:T(8,128)S(1)}, u32[]{:S(2)}, u32[]{:S(2)}) collective-permute-start(f32[56,128]{1,0:T(8,128)S(1)} %fusion.2), channel_id=1, source_target_pairs={{0,5},{1,4},{2,7},{3,6},{4,1},{5,0},{6,3},{7,2},{8,13},{9,12},{10,... | collective-permute-start | bytes 86024 | tf_op jit(solution)/shard_map/ppermute | solution.py:226
  32.3 1.9 %collective-permute-done.9 = f32[56,128]{1,0:T(8,128)S(1)} collective-permute-done((f32[56,128]{1,0:T(8,128)S(1)}, f32[56,128]{1,0:T(8,128)S(1)}, u32[]{:S(2)}, u32[]{:S(2)}) %collective-permute-start.9) | collective-permute-done | bytes 28704 | tf_op jit(solution)/shard_map/ppermute | solution.py:226
  34.2 1.1 %collective-permute-start.10 = (f32[40,128]{1,0:T(8,128)S(1)}, f32[40,128]{1,0:T(8,128)S(1)}, u32[]{:S(2)}, u32[]{:S(2)}) collective-permute-start(f32[40,128]{1,0:T(8,128)S(1)} %fusion.6), channel_id=1, source_target_pairs={{0,9},{1,8},{2,11},{3,10},{4,13},{5,12},{6,15},{7,14},{8,1},{9,0},... | collective-permute-start | bytes 61448 | tf_op jit(solution)/shard_map/ppermute | solution.py:226
  35.3 1.3 %collective-permute-start.12 = (f32[40,128]{1,0:T(8,128)S(1)}, f32[40,128]{1,0:T(8,128)S(1)}, u32[]{:S(2)}, u32[]{:S(2)}) collective-permute-start(f32[40,128]{1,0:T(8,128)S(1)} %fusion.6), channel_id=1, source_target_pairs={{0,24},{1,25},{2,26},{3,27},{4,28},{5,29},{6,30},{7,31},{8,16},{9,... | collective-permute-start | bytes 61448 | tf_op jit(solution)/shard_map/ppermute | solution.py:226
  36.6 0.6 %collective-permute-start.11 = (f32[40,128]{1,0:T(8,128)S(1)}, f32[40,128]{1,0:T(8,128)S(1)}, u32[]{:S(2)}, u32[]{:S(2)}) collective-permute-start(f32[40,128]{1,0:T(8,128)S(1)} %fusion.6), channel_id=1, source_target_pairs={{0,17},{1,16},{2,19},{3,18},{4,21},{5,20},{6,23},{7,22},{8,25},{9,... | collective-permute-start | bytes 61448 | tf_op jit(solution)/shard_map/ppermute | solution.py:226
  37.2 0.3 collective-permute-done.10
  37.5 2.5 %collective-permute-done.12 = f32[40,128]{1,0:T(8,128)S(1)} collective-permute-done((f32[40,128]{1,0:T(8,128)S(1)}, f32[40,128]{1,0:T(8,128)S(1)}, u32[]{:S(2)}, u32[]{:S(2)}) %collective-permute-start.12) | collective-permute-done | bytes 20512 | tf_op jit(solution)/shard_map/ppermute | solution.py:226
  40.0 0.0 collective-permute-done.11
  40.1 0.1 collective-permute-start.13
  40.2 1.2 %collective-permute-done.13.other_ref = f32[72,128]{1,0:T(8,128)S(1)} collective-permute-done((f32[72,128]{1,0:T(8,128)S(1)}, f32[72,128]{1,0:T(8,128)S(1)}, u32[]{:S(2)}, u32[]{:S(2)}) %collective-permute-start.13) | collective-permute-done | bytes 36896 | tf_op jit(solution)/shard_map/ppermute | solution.py:226
  41.4 1.9 %last.1 = (f32[64,1024]{1,0:T(8,128)}, f32[64,1024]{1,0:T(8,128)}) custom-call(s32[1,1024]{1,0:T(1,128)S(1)} %get-tuple-element.18.order_ref, f32[96,128]{1,0:T(8,128)S(1)} %collective-permute-done.7.zero_ref, f32[72,128]{1,0:T(8,128)S(1)} %constant_dynamic-update-slice_fusion.5.own_ref, f32[72,128]{1,0:T(8,128)S(1)} %collective-permute-done.13.other_ref, ...), custom_call_target="tpu_custom_call" | custom-call | tf_op jit(solution)/shard_map/last/pallas_call | solution.py:313
  (34 shorter events, 0.4 us)
Async XLA Ops:
  3.1 3.8 %collective-permute-start = (f32[96,128]{1,0:T(8,128)S(1)}, f32[96,128]{1,0:T(8,128)S(1)}, u32[]{:S(2)}, u32[]{:S(2)}) collective-permute-start(f32[96,128]{1,0:T(8,128)S(1)} %get-tuple-element.19), channel_id=1, source_target_pairs={{0,1},{1,0},{2,3},{3,2},{4,5},{5,4},{6,7},{7,6},{8,9},{9,8},{10,11... | collective-permute-start | bytes 147464 | tf_op jit(solution)/shard_map/ppermute | solution.py:226
  3.6 2.2 %copy-start = (f32[1024,1024]{1,0:T(8,128)S(1)}, f32[1024,1024]{1,0:T(8,128)}, u32[]{:S(2)}) copy-start(f32[1024,1024]{1,0:T(8,128)} %d_ref.1) | copy-start | bytes 12582916
  7.0 4.6 %collective-permute-start.1 = (f32[72,128]{1,0:T(8,128)S(1)}, f32[72,128]{1,0:T(8,128)S(1)}, u32[]{:S(2)}, u32[]{:S(2)}) collective-permute-start(f32[72,128]{1,0:T(8,128)S(1)} %pad_maximum_fusion), channel_id=1, source_target_pairs={{0,3},{1,2},{2,1},{3,0},{4,7},{5,6},{6,5},{7,4},{8,11},{9,10},{10,... | collective-permute-start | bytes 110600 | tf_op jit(solution)/shard_map/ppermute | solution.py:226
  11.6 4.3 %collective-permute-start.2 = (f32[56,128]{1,0:T(8,128)S(1)}, f32[56,128]{1,0:T(8,128)S(1)}, u32[]{:S(2)}, u32[]{:S(2)}) collective-permute-start(f32[56,128]{1,0:T(8,128)S(1)} %fusion.5), channel_id=1, source_target_pairs={{0,5},{1,4},{2,7},{3,6},{4,1},{5,0},{6,3},{7,2},{8,13},{9,12},{10,... | collective-permute-start | bytes 86024 | tf_op jit(solution)/shard_map/ppermute | solution.py:226
  15.9 3.3 %collective-permute-start.3 = (f32[40,128]{1,0:T(8,128)S(1)}, f32[40,128]{1,0:T(8,128)S(1)}, u32[]{:S(2)}, u32[]{:S(2)}) collective-permute-start(f32[40,128]{1,0:T(8,128)S(1)} %fusion.7), channel_id=1, source_target_pairs={{0,9},{1,8},{2,11},{3,10},{4,13},{5,12},{6,15},{7,14},{8,1},{9,0},... | collective-permute-start | bytes 61448 | tf_op jit(solution)/shard_map/ppermute | solution.py:226
  17.4 4.8 %collective-permute-start.5 = (f32[40,128]{1,0:T(8,128)S(1)}, f32[40,128]{1,0:T(8,128)S(1)}, u32[]{:S(2)}, u32[]{:S(2)}) collective-permute-start(f32[40,128]{1,0:T(8,128)S(1)} %fusion.7), channel_id=1, source_target_pairs={{0,24},{1,25},{2,26},{3,27},{4,28},{5,29},{6,30},{7,31},{8,16},{9,... | collective-permute-start | bytes 61448 | tf_op jit(solution)/shard_map/ppermute | solution.py:226
  18.9 3.6 %collective-permute-start.4 = (f32[40,128]{1,0:T(8,128)S(1)}, f32[40,128]{1,0:T(8,128)S(1)}, u32[]{:S(2)}, u32[]{:S(2)}) collective-permute-start(f32[40,128]{1,0:T(8,128)S(1)} %fusion.7), channel_id=1, source_target_pairs={{0,17},{1,16},{2,19},{3,18},{4,21},{5,20},{6,23},{7,22},{8,25},{9,... | collective-permute-start | bytes 61448 | tf_op jit(solution)/shard_map/ppermute | solution.py:226
  22.6 1.3 %collective-permute-start.6 = (f32[72,128]{1,0:T(8,128)S(1)}, f32[72,128]{1,0:T(8,128)S(1)}, u32[]{:S(2)}, u32[]{:S(2)}) collective-permute-start(f32[72,128]{1,0:T(8,128)S(1)} %constant_dynamic-update-slice_fusion.own_ref.old_own_ref), channel_id=1, source_target_pairs={{0,1},{1,0},{2,3},{3,2},{4,5},{5,4},{6,7},{7,6},{8,9},{9,8},{10,11... | collective-permute-start | bytes 110600 | tf_op jit(solution)/shard_map/ppermute | solution.py:226
  25.0 1.3 %collective-permute-start.7 = (f32[96,128]{1,0:T(8,128)S(1)}, f32[96,128]{1,0:T(8,128)S(1)}, u32[]{:S(2)}, u32[]{:S(2)}) collective-permute-start(f32[96,128]{1,0:T(8,128)S(1)} %get-tuple-element.26), channel_id=1, source_target_pairs={{0,1},{1,0},{2,3},{3,2},{4,5},{5,4},{6,7},{7,6},{8,9},{9,8},{10,11... | collective-permute-start | bytes 147464 | tf_op jit(solution)/shard_map/ppermute | solution.py:226
  26.3 3.5 %collective-permute-start.8 = (f32[72,128]{1,0:T(8,128)S(1)}, f32[72,128]{1,0:T(8,128)S(1)}, u32[]{:S(2)}, u32[]{:S(2)}) collective-permute-start(f32[72,128]{1,0:T(8,128)S(1)} %pad_maximum_fusion.1), channel_id=1, source_target_pairs={{0,3},{1,2},{2,1},{3,0},{4,7},{5,6},{6,5},{7,4},{8,11},{9,10},{10,... | collective-permute-start | bytes 110600 | tf_op jit(solution)/shard_map/ppermute | solution.py:226
  29.9 4.3 %collective-permute-start.9 = (f32[56,128]{1,0:T(8,128)S(1)}, f32[56,128]{1,0:T(8,128)S(1)}, u32[]{:S(2)}, u32[]{:S(2)}) collective-permute-start(f32[56,128]{1,0:T(8,128)S(1)} %fusion.2), channel_id=1, source_target_pairs={{0,5},{1,4},{2,7},{3,6},{4,1},{5,0},{6,3},{7,2},{8,13},{9,12},{10,... | collective-permute-start | bytes 86024 | tf_op jit(solution)/shard_map/ppermute | solution.py:226
  34.2 3.3 %collective-permute-start.10 = (f32[40,128]{1,0:T(8,128)S(1)}, f32[40,128]{1,0:T(8,128)S(1)}, u32[]{:S(2)}, u32[]{:S(2)}) collective-permute-start(f32[40,128]{1,0:T(8,128)S(1)} %fusion.6), channel_id=1, source_target_pairs={{0,9},{1,8},{2,11},{3,10},{4,13},{5,12},{6,15},{7,14},{8,1},{9,0},... | collective-permute-start | bytes 61448 | tf_op jit(solution)/shard_map/ppermute | solution.py:226
  35.3 4.7 %collective-permute-start.12 = (f32[40,128]{1,0:T(8,128)S(1)}, f32[40,128]{1,0:T(8,128)S(1)}, u32[]{:S(2)}, u32[]{:S(2)}) collective-permute-start(f32[40,128]{1,0:T(8,128)S(1)} %fusion.6), channel_id=1, source_target_pairs={{0,24},{1,25},{2,26},{3,27},{4,28},{5,29},{6,30},{7,31},{8,16},{9,... | collective-permute-start | bytes 61448 | tf_op jit(solution)/shard_map/ppermute | solution.py:226
  36.6 3.5 %collective-permute-start.11 = (f32[40,128]{1,0:T(8,128)S(1)}, f32[40,128]{1,0:T(8,128)S(1)}, u32[]{:S(2)}, u32[]{:S(2)}) collective-permute-start(f32[40,128]{1,0:T(8,128)S(1)} %fusion.6), channel_id=1, source_target_pairs={{0,17},{1,16},{2,19},{3,18},{4,21},{5,20},{6,23},{7,22},{8,25},{9,... | collective-permute-start | bytes 61448 | tf_op jit(solution)/shard_map/ppermute | solution.py:226
  40.1 1.3 %collective-permute-start.13 = (f32[72,128]{1,0:T(8,128)S(1)}, f32[72,128]{1,0:T(8,128)S(1)}, u32[]{:S(2)}, u32[]{:S(2)}) collective-permute-start(f32[72,128]{1,0:T(8,128)S(1)} %constant_dynamic-update-slice_fusion.5.own_ref), channel_id=1, source_target_pairs={{0,1},{1,0},{2,3},{3,2},{4,5},{5,4},{6,7},{7,6},{8,9},{9,8},{10,11... | collective-permute-start | bytes 110600 | tf_op jit(solution)/shard_map/ppermute | solution.py:226

commit v4 on v3

--- a/solution.py
+++ b/solution.py
@@ -293,7 +293,7 @@
     scratch = [pltpu.VMEM(right_side.shape, F32), pltpu.VMEM(factors.shape, F32), pltpu.SemaphoreType.DMA((3,))]
     b, first, mine, qhi, qlo, order = call(
         start_kernel, "start", (field, message, own, basis, basis, jax.ShapeDtypeStruct((1, leaf), jnp.int32)),
-        [HBM] * 3, scratch)(*pinned)
+        [HBM] * 3, scratch, FLOPS)(*pinned)
     kept = {}
 
     def first_tail():

time: 43.5 us -> 41.4 us (0.952)
  local copies, waits for them, and re-layouts: 2.19 us -> 0.01 us
    unnamed x2, local copies, waits for them, and re-layouts: 2.19 us -> 0.01 us
  transfers between devices with their start and end apart: 14 -> 14, of which waited for: 12 -> 12; matrix products, arithmetic and copies ran while one was open for 0% -> 0% of each run, Pallas kernels for 4% -> 5%
where the time goes in v4:
time: 41.4 us; the launch traced here: 41.3 us
  starting transfers between devices  16.5 us (40%)
  waiting for transfers between devices  16.1 us (39%)
  Pallas kernels  7.57 us (18%)
  between operations  0.74 us (2%)
    ppermute x14, starting transfers between devices, swapped(): lax.ppermute(value, AXES, [(source, source ^ mask) for source in range(co...  16.5 us
    ppermute x14, waiting for transfers between devices, swapped(): lax.ppermute(value, AXES, [(source, source ^ mask) for source in range(co...  16.1 us
    pallas_call x1, Pallas kernels, local(): call(start_kernel, 'start', (field, message, own, basis, basis, jax.Shape...  2.56 us
    pallas_call x1, Pallas kernels, local(): call(last_kernel, 'last', (field, field), [VMEM] * 12)  1.94 us
    pallas_call x1, Pallas kernels, local(): call(step_kernel, 'step', (field, field, message, own), [VMEM] * 7)  1.12 us
    pallas_call x1, Pallas kernels, first_tail(): call(near_kernel, 'near', (field, tail, matrix, matrix), [VMEM] * 2, flop...  1.08 us
    pallas_call x1, Pallas kernels, next_tail(): call(again_kernel, 'again', (field, tail), [VMEM] * 3, flops=FLOPS)  0.86 us
  transfers between devices with their start and end apart: 14, of which 12 were waited for; matrix products, arithmetic and copies ran while one was open for 0% of the time, Pallas kernels for 5%

profile of v4, /device:TPU:0, one launch (start us, length us, event | category | flops | bytes accessed | tf_op | source)
XLA Modules:
  0.0 41.3 jit_solution(5347801200677749210)
XLA Ops:
  0.6 0.0 copy-start
  0.6 2.6 %start.1 = (f32[64,1024]{1,0:T(8,128)S(1)}, f32[96,128]{1,0:T(8,128)S(1)}, f32[64,128]{1,0:T(8,128)S(1)}, bf16[320,1024]{1,0:T(8,128)(2,1)S(1)}, bf16[320,1024]{1,0:T(8,128)(2,1)S(1)}, /*index=5*/s32[1,1024]{1,0:T(1,128)S(1)}) custom-call(s32[1,1024]{1,0:T(1,128)} %bitcast.17, f32[64,1024]{1,0:T(8,128)} %rs_hbm.1, f32[5,64,1024]{2,1,0:T(8,128)} %f_hbm.1), custom_call_target="tpu_custom_call" | custom-call | flops 2000000000 | tf_op jit(solution)/shard_map/start/pallas_call | solution.py:294
  3.2 0.6 %collective-permute-start = (f32[96,128]{1,0:T(8,128)S(1)}, f32[96,128]{1,0:T(8,128)S(1)}, u32[]{:S(2)}, u32[]{:S(2)}) collective-permute-start(f32[96,128]{1,0:T(8,128)S(1)} %get-tuple-element.19), channel_id=1, source_target_pairs={{0,1},{1,0},{2,3},{3,2},{4,5},{5,4},{6,7},{7,6},{8,9},{9,8},{10,11... | collective-permute-start | bytes 147464 | tf_op jit(solution)/shard_map/ppermute | solution.py:226
  3.8 0.0 copy-done
  3.8 1.1 %near.1 = (f32[64,1024]{1,0:T(8,128)S(1)}, f32[8,128]{1,0:T(8,128)S(1)}, bf16[1024,1024]{1,0:T(8,128)(2,1)S(1)}, bf16[1024,1024]{1,0:T(8,128)(2,1)S(1)}) custom-call(f32[64,1024]{1,0:T(8,128)S(1)} %get-tuple-element.21.b_ref, f32[1024,1024]{1,0:T(8,128)S(1)} %copy-done), custom_call_target="tpu_custom_call" | custom-call | flops 2000000000 | tf_op jit(solution)/shard_map/near/pallas_call | solution.py:300
  4.8 0.0 collective-permute-done.zero_ref
  4.9 2.7 %collective-permute-start.1 = (f32[72,128]{1,0:T(8,128)S(1)}, f32[72,128]{1,0:T(8,128)S(1)}, u32[]{:S(2)}, u32[]{:S(2)}) collective-permute-start(f32[72,128]{1,0:T(8,128)S(1)} %pad_maximum_fusion), channel_id=1, source_target_pairs={{0,3},{1,2},{2,1},{3,0},{4,7},{5,6},{6,5},{7,4},{8,11},{9,10},{10,... | collective-permute-start | bytes 110600 | tf_op jit(solution)/shard_map/ppermute | solution.py:226
  7.7 1.7 %collective-permute-done.1 = f32[72,128]{1,0:T(8,128)S(1)} collective-permute-done((f32[72,128]{1,0:T(8,128)S(1)}, f32[72,128]{1,0:T(8,128)S(1)}, u32[]{:S(2)}, u32[]{:S(2)}) %collective-permute-start.1) | collective-permute-done | bytes 36896 | tf_op jit(solution)/shard_map/ppermute | solution.py:226
  9.4 2.7 %collective-permute-start.2 = (f32[56,128]{1,0:T(8,128)S(1)}, f32[56,128]{1,0:T(8,128)S(1)}, u32[]{:S(2)}, u32[]{:S(2)}) collective-permute-start(f32[56,128]{1,0:T(8,128)S(1)} %fusion.5), channel_id=1, source_target_pairs={{0,5},{1,4},{2,7},{3,6},{4,1},{5,0},{6,3},{7,2},{8,13},{9,12},{10,... | collective-permute-start | bytes 86024 | tf_op jit(solution)/shard_map/ppermute | solution.py:226
  12.2 1.6 %collective-permute-done.2 = f32[56,128]{1,0:T(8,128)S(1)} collective-permute-done((f32[56,128]{1,0:T(8,128)S(1)}, f32[56,128]{1,0:T(8,128)S(1)}, u32[]{:S(2)}, u32[]{:S(2)}) %collective-permute-start.2) | collective-permute-done | bytes 28704 | tf_op jit(solution)/shard_map/ppermute | solution.py:226
  13.8 1.6 %collective-permute-start.3 = (f32[40,128]{1,0:T(8,128)S(1)}, f32[40,128]{1,0:T(8,128)S(1)}, u32[]{:S(2)}, u32[]{:S(2)}) collective-permute-start(f32[40,128]{1,0:T(8,128)S(1)} %fusion.7), channel_id=1, source_target_pairs={{0,9},{1,8},{2,11},{3,10},{4,13},{5,12},{6,15},{7,14},{8,1},{9,0},... | collective-permute-start | bytes 61448 | tf_op jit(solution)/shard_map/ppermute | solution.py:226
  15.4 1.5 %collective-permute-start.5 = (f32[40,128]{1,0:T(8,128)S(1)}, f32[40,128]{1,0:T(8,128)S(1)}, u32[]{:S(2)}, u32[]{:S(2)}) collective-permute-start(f32[40,128]{1,0:T(8,128)S(1)} %fusion.7), channel_id=1, source_target_pairs={{0,24},{1,25},{2,26},{3,27},{4,28},{5,29},{6,30},{7,31},{8,16},{9,... | collective-permute-start | bytes 61448 | tf_op jit(solution)/shard_map/ppermute | solution.py:226
  16.9 0.0 collective-permute-start.4
  16.9 0.2 collective-permute-done.3
  17.1 3.0 %collective-permute-done.5 = f32[40,128]{1,0:T(8,128)S(1)} collective-permute-done((f32[40,128]{1,0:T(8,128)S(1)}, f32[40,128]{1,0:T(8,128)S(1)}, u32[]{:S(2)}, u32[]{:S(2)}) %collective-permute-start.5) | collective-permute-done | bytes 20512 | tf_op jit(solution)/shard_map/ppermute | solution.py:226
  20.1 0.4 %collective-permute-done.4 = f32[40,128]{1,0:T(8,128)S(1)} collective-permute-done((f32[40,128]{1,0:T(8,128)S(1)}, f32[40,128]{1,0:T(8,128)S(1)}, u32[]{:S(2)}, u32[]{:S(2)}) %collective-permute-start.4) | collective-permute-done | bytes 20512 | tf_op jit(solution)/shard_map/ppermute | solution.py:226
  20.6 0.2 collective-permute-start.6
  20.7 1.1 %collective-permute-done.6.other_ref.old_other_ref = f32[72,128]{1,0:T(8,128)S(1)} collective-permute-done((f32[72,128]{1,0:T(8,128)S(1)}, f32[72,128]{1,0:T(8,128)S(1)}, u32[]{:S(2)}, u32[]{:S(2)}) %collective-permute-start.6) | collective-permute-done | bytes 36896 | tf_op jit(solution)/shard_map/ppermute | solution.py:226
  21.8 1.1 %step.1 = (f32[64,1024]{1,0:T(8,128)S(1)}, f32[64,1024]{1,0:T(8,128)S(1)}, f32[96,128]{1,0:T(8,128)S(1)}, f32[64,128]{1,0:T(8,128)S(1)}) custom-call(f32[96,128]{1,0:T(8,128)S(1)} %collective-permute-done.zero_ref, f32[72,128]{1,0:T(8,128)S(1)} %constant_dynamic-update-slice_fusion.own_ref.old_own_ref, ...), custom_call_target="tpu_custom_call" | custom-call | tf_op jit(solution)/shard_map/step/pallas_call | solution.py:305
  23.0 0.2 collective-permute-start.7
  23.2 0.9 %again.1 = (f32[64,1024]{1,0:T(8,128)S(1)}, f32[8,128]{1,0:T(8,128)S(1)}) custom-call(f32[64,1024]{1,0:T(8,128)S(1)} %get-tuple-element.28.r_ref, bf16[1024,1024]{1,0:T(8,128)(2,1)S(1)} %get-tuple-element.29.dhi_ref, bf16[1024,1024]{1,0:T(8,128)(2,1)S(1)} %get-tuple-element.30.dlo_ref), custom_call_target="tpu_custom_call" | custom-call | flops 2000000000 | tf_op jit(solution)/shard_map/again/pallas_call | solution.py:309
  24.1 0.2 collective-permute-done.7.zero_ref
  24.3 1.4 %collective-permute-start.8 = (f32[72,128]{1,0:T(8,128)S(1)}, f32[72,128]{1,0:T(8,128)S(1)}, u32[]{:S(2)}, u32[]{:S(2)}) collective-permute-start(f32[72,128]{1,0:T(8,128)S(1)} %pad_maximum_fusion.1), channel_id=1, source_target_pairs={{0,3},{1,2},{2,1},{3,0},{4,7},{5,6},{6,5},{7,4},{8,11},{9,10},{10,... | collective-permute-start | bytes 110600 | tf_op jit(solution)/shard_map/ppermute | solution.py:226
  25.7 2.1 %collective-permute-done.8 = f32[72,128]{1,0:T(8,128)S(1)} collective-permute-done((f32[72,128]{1,0:T(8,128)S(1)}, f32[72,128]{1,0:T(8,128)S(1)}, u32[]{:S(2)}, u32[]{:S(2)}) %collective-permute-start.8) | collective-permute-done | bytes 36896 | tf_op jit(solution)/shard_map/ppermute | solution.py:226
  27.9 2.4 %collective-permute-start.9 = (f32[56,128]{1,0:T(8,128)S(1)}, f32[56,128]{1,0:T(8,128)S(1)}, u32[]{:S(2)}, u32[]{:S(2)}) collective-permute-start(f32[56,128]{1,0:T(8,128)S(1)} %fusion.2), channel_id=1, source_target_pairs={{0,5},{1,4},{2,7},{3,6},{4,1},{5,0},{6,3},{7,2},{8,13},{9,12},{10,... | collective-permute-start | bytes 86024 | tf_op jit(solution)/shard_map/ppermute | solution.py:226
  30.3 1.8 %collective-permute-done.9 = f32[56,128]{1,0:T(8,128)S(1)} collective-permute-done((f32[56,128]{1,0:T(8,128)S(1)}, f32[56,128]{1,0:T(8,128)S(1)}, u32[]{:S(2)}, u32[]{:S(2)}) %collective-permute-start.9) | collective-permute-done | bytes 28704 | tf_op jit(solution)/shard_map/ppermute | solution.py:226
  32.2 1.1 %collective-permute-start.10 = (f32[40,128]{1,0:T(8,128)S(1)}, f32[40,128]{1,0:T(8,128)S(1)}, u32[]{:S(2)}, u32[]{:S(2)}) collective-permute-start(f32[40,128]{1,0:T(8,128)S(1)} %fusion.6), channel_id=1, source_target_pairs={{0,9},{1,8},{2,11},{3,10},{4,13},{5,12},{6,15},{7,14},{8,1},{9,0},... | collective-permute-start | bytes 61448 | tf_op jit(solution)/shard_map/ppermute | solution.py:226
  33.2 1.3 %collective-permute-start.12 = (f32[40,128]{1,0:T(8,128)S(1)}, f32[40,128]{1,0:T(8,128)S(1)}, u32[]{:S(2)}, u32[]{:S(2)}) collective-permute-start(f32[40,128]{1,0:T(8,128)S(1)} %fusion.6), channel_id=1, source_target_pairs={{0,24},{1,25},{2,26},{3,27},{4,28},{5,29},{6,30},{7,31},{8,16},{9,... | collective-permute-start | bytes 61448 | tf_op jit(solution)/shard_map/ppermute | solution.py:226
  34.5 0.6 %collective-permute-start.11 = (f32[40,128]{1,0:T(8,128)S(1)}, f32[40,128]{1,0:T(8,128)S(1)}, u32[]{:S(2)}, u32[]{:S(2)}) collective-permute-start(f32[40,128]{1,0:T(8,128)S(1)} %fusion.6), channel_id=1, source_target_pairs={{0,17},{1,16},{2,19},{3,18},{4,21},{5,20},{6,23},{7,22},{8,25},{9,... | collective-permute-start | bytes 61448 | tf_op jit(solution)/shard_map/ppermute | solution.py:226
  35.2 0.3 collective-permute-done.10
  35.5 2.5 %collective-permute-done.12 = f32[40,128]{1,0:T(8,128)S(1)} collective-permute-done((f32[40,128]{1,0:T(8,128)S(1)}, f32[40,128]{1,0:T(8,128)S(1)}, u32[]{:S(2)}, u32[]{:S(2)}) %collective-permute-start.12) | collective-permute-done | bytes 20512 | tf_op jit(solution)/shard_map/ppermute | solution.py:226
  38.0 0.0 collective-permute-done.11
  38.1 0.1 collective-permute-start.13
  38.2 1.2 %collective-permute-done.13.other_ref = f32[72,128]{1,0:T(8,128)S(1)} collective-permute-done((f32[72,128]{1,0:T(8,128)S(1)}, f32[72,128]{1,0:T(8,128)S(1)}, u32[]{:S(2)}, u32[]{:S(2)}) %collective-permute-start.13) | collective-permute-done | bytes 36896 | tf_op jit(solution)/shard_map/ppermute | solution.py:226
  39.3 1.9 %last.1 = (f32[64,1024]{1,0:T(8,128)}, f32[64,1024]{1,0:T(8,128)}) custom-call(s32[1,1024]{1,0:T(1,128)S(1)} %get-tuple-element.18.order_ref, f32[96,128]{1,0:T(8,128)S(1)} %collective-permute-done.7.zero_ref, f32[72,128]{1,0:T(8,128)S(1)} %constant_dynamic-update-slice_fusion.5.own_ref, f32[72,128]{1,0:T(8,128)S(1)} %collective-permute-done.13.other_ref, ...), custom_call_target="tpu_custom_call" | custom-call | tf_op jit(solution)/shard_map/last/pallas_call | solution.py:313
  (34 shorter events, 0.4 us)
Async XLA Ops:
  0.6 3.1 %copy-start = (f32[1024,1024]{1,0:T(8,128)S(1)}, f32[1024,1024]{1,0:T(8,128)}, u32[]{:S(2)}) copy-start(f32[1024,1024]{1,0:T(8,128)} %d_ref.1) | copy-start | bytes 12582916
  3.2 1.6 %collective-permute-start = (f32[96,128]{1,0:T(8,128)S(1)}, f32[96,128]{1,0:T(8,128)S(1)}, u32[]{:S(2)}, u32[]{:S(2)}) collective-permute-start(f32[96,128]{1,0:T(8,128)S(1)} %get-tuple-element.19), channel_id=1, source_target_pairs={{0,1},{1,0},{2,3},{3,2},{4,5},{5,4},{6,7},{7,6},{8,9},{9,8},{10,11... | collective-permute-start | bytes 147464 | tf_op jit(solution)/shard_map/ppermute | solution.py:226
  4.9 4.5 %collective-permute-start.1 = (f32[72,128]{1,0:T(8,128)S(1)}, f32[72,128]{1,0:T(8,128)S(1)}, u32[]{:S(2)}, u32[]{:S(2)}) collective-permute-start(f32[72,128]{1,0:T(8,128)S(1)} %pad_maximum_fusion), channel_id=1, source_target_pairs={{0,3},{1,2},{2,1},{3,0},{4,7},{5,6},{6,5},{7,4},{8,11},{9,10},{10,... | collective-permute-start | bytes 110600 | tf_op jit(solution)/shard_map/ppermute | solution.py:226
  9.4 4.3 %collective-permute-start.2 = (f32[56,128]{1,0:T(8,128)S(1)}, f32[56,128]{1,0:T(8,128)S(1)}, u32[]{:S(2)}, u32[]{:S(2)}) collective-permute-start(f32[56,128]{1,0:T(8,128)S(1)} %fusion.5), channel_id=1, source_target_pairs={{0,5},{1,4},{2,7},{3,6},{4,1},{5,0},{6,3},{7,2},{8,13},{9,12},{10,... | collective-permute-start | bytes 86024 | tf_op jit(solution)/shard_map/ppermute | solution.py:226
  13.8 3.3 %collective-permute-start.3 = (f32[40,128]{1,0:T(8,128)S(1)}, f32[40,128]{1,0:T(8,128)S(1)}, u32[]{:S(2)}, u32[]{:S(2)}) collective-permute-start(f32[40,128]{1,0:T(8,128)S(1)} %fusion.7), channel_id=1, source_target_pairs={{0,9},{1,8},{2,11},{3,10},{4,13},{5,12},{6,15},{7,14},{8,1},{9,0},... | collective-permute-start | bytes 61448 | tf_op jit(solution)/shard_map/ppermute | solution.py:226
  15.4 4.7 %collective-permute-start.5 = (f32[40,128]{1,0:T(8,128)S(1)}, f32[40,128]{1,0:T(8,128)S(1)}, u32[]{:S(2)}, u32[]{:S(2)}) collective-permute-start(f32[40,128]{1,0:T(8,128)S(1)} %fusion.7), channel_id=1, source_target_pairs={{0,24},{1,25},{2,26},{3,27},{4,28},{5,29},{6,30},{7,31},{8,16},{9,... | collective-permute-start | bytes 61448 | tf_op jit(solution)/shard_map/ppermute | solution.py:226
  16.9 3.6 %collective-permute-start.4 = (f32[40,128]{1,0:T(8,128)S(1)}, f32[40,128]{1,0:T(8,128)S(1)}, u32[]{:S(2)}, u32[]{:S(2)}) collective-permute-start(f32[40,128]{1,0:T(8,128)S(1)} %fusion.7), channel_id=1, source_target_pairs={{0,17},{1,16},{2,19},{3,18},{4,21},{5,20},{6,23},{7,22},{8,25},{9,... | collective-permute-start | bytes 61448 | tf_op jit(solution)/shard_map/ppermute | solution.py:226
  20.6 1.3 %collective-permute-start.6 = (f32[72,128]{1,0:T(8,128)S(1)}, f32[72,128]{1,0:T(8,128)S(1)}, u32[]{:S(2)}, u32[]{:S(2)}) collective-permute-start(f32[72,128]{1,0:T(8,128)S(1)} %constant_dynamic-update-slice_fusion.own_ref.old_own_ref), channel_id=1, source_target_pairs={{0,1},{1,0},{2,3},{3,2},{4,5},{5,4},{6,7},{7,6},{8,9},{9,8},{10,11... | collective-permute-start | bytes 110600 | tf_op jit(solution)/shard_map/ppermute | solution.py:226
  23.0 1.3 %collective-permute-start.7 = (f32[96,128]{1,0:T(8,128)S(1)}, f32[96,128]{1,0:T(8,128)S(1)}, u32[]{:S(2)}, u32[]{:S(2)}) collective-permute-start(f32[96,128]{1,0:T(8,128)S(1)} %get-tuple-element.26), channel_id=1, source_target_pairs={{0,1},{1,0},{2,3},{3,2},{4,5},{5,4},{6,7},{7,6},{8,9},{9,8},{10,11... | collective-permute-start | bytes 147464 | tf_op jit(solution)/shard_map/ppermute | solution.py:226
  24.3 3.5 %collective-permute-start.8 = (f32[72,128]{1,0:T(8,128)S(1)}, f32[72,128]{1,0:T(8,128)S(1)}, u32[]{:S(2)}, u32[]{:S(2)}) collective-permute-start(f32[72,128]{1,0:T(8,128)S(1)} %pad_maximum_fusion.1), channel_id=1, source_target_pairs={{0,3},{1,2},{2,1},{3,0},{4,7},{5,6},{6,5},{7,4},{8,11},{9,10},{10,... | collective-permute-start | bytes 110600 | tf_op jit(solution)/shard_map/ppermute | solution.py:226
  27.9 4.3 %collective-permute-start.9 = (f32[56,128]{1,0:T(8,128)S(1)}, f32[56,128]{1,0:T(8,128)S(1)}, u32[]{:S(2)}, u32[]{:S(2)}) collective-permute-start(f32[56,128]{1,0:T(8,128)S(1)} %fusion.2), channel_id=1, source_target_pairs={{0,5},{1,4},{2,7},{3,6},{4,1},{5,0},{6,3},{7,2},{8,13},{9,12},{10,... | collective-permute-start | bytes 86024 | tf_op jit(solution)/shard_map/ppermute | solution.py:226
  32.2 3.3 %collective-permute-start.10 = (f32[40,128]{1,0:T(8,128)S(1)}, f32[40,128]{1,0:T(8,128)S(1)}, u32[]{:S(2)}, u32[]{:S(2)}) collective-permute-start(f32[40,128]{1,0:T(8,128)S(1)} %fusion.6), channel_id=1, source_target_pairs={{0,9},{1,8},{2,11},{3,10},{4,13},{5,12},{6,15},{7,14},{8,1},{9,0},... | collective-permute-start | bytes 61448 | tf_op jit(solution)/shard_map/ppermute | solution.py:226
  33.2 4.7 %collective-permute-start.12 = (f32[40,128]{1,0:T(8,128)S(1)}, f32[40,128]{1,0:T(8,128)S(1)}, u32[]{:S(2)}, u32[]{:S(2)}) collective-permute-start(f32[40,128]{1,0:T(8,128)S(1)} %fusion.6), channel_id=1, source_target_pairs={{0,24},{1,25},{2,26},{3,27},{4,28},{5,29},{6,30},{7,31},{8,16},{9,... | collective-permute-start | bytes 61448 | tf_op jit(solution)/shard_map/ppermute | solution.py:226
  34.5 3.4 %collective-permute-start.11 = (f32[40,128]{1,0:T(8,128)S(1)}, f32[40,128]{1,0:T(8,128)S(1)}, u32[]{:S(2)}, u32[]{:S(2)}) collective-permute-start(f32[40,128]{1,0:T(8,128)S(1)} %fusion.6), channel_id=1, source_target_pairs={{0,17},{1,16},{2,19},{3,18},{4,21},{5,20},{6,23},{7,22},{8,25},{9,... | collective-permute-start | bytes 61448 | tf_op jit(solution)/shard_map/ppermute | solution.py:226
  38.1 1.3 %collective-permute-start.13 = (f32[72,128]{1,0:T(8,128)S(1)}, f32[72,128]{1,0:T(8,128)S(1)}, u32[]{:S(2)}, u32[]{:S(2)}) collective-permute-start(f32[72,128]{1,0:T(8,128)S(1)} %constant_dynamic-update-slice_fusion.5.own_ref), channel_id=1, source_target_pairs={{0,1},{1,0},{2,3},{3,2},{4,5},{5,4},{6,7},{7,6},{8,9},{9,8},{10,11... | collective-permute-start | bytes 110600 | tf_op jit(solution)/shard_map/ppermute | solution.py:226
